TPU v7x, 32 devices: a whole 2x2x4 slice. The times are simulated.
32 devices in a mesh: lat: 8 (over z, x), lev: 4 (over y, core).
Axes of the slice: x: 2, y: 2, z: 4, core: 2. Of those that a mesh axis runs over, the one named last changes fastest.
Arguments:
- fourier: bfloat16 [1280, 640, 1024], P('lat', None, 'lev'), may hold values from -6 to 6
- legendre: bfloat16 [640, 2, 640, 320], P('lat', None, 'lev'), may hold values from -0.25 to 0.25
- owner: int32 [640], replicated, may hold values from 0 to 7, as said below
Outputs:
- spectral: bfloat16 [640, 2, 320, 1024], P('lat', None, None, 'lev')
Inputs may be any that keep to these rules, and one draw needn't show every extreme that they name: `owner`: each index along lat is named by exactly 80 wavenumbers.
All inputs are finite; a program needn't handle non-finite values.
Results may differ from a plain program's by a relative error of at most 0.0051.
Values may be sent and summed in bfloat16 or wider, within the bound.
No kernel may reach another device: no remote copies, remote signals or barrier semaphores. Data moves between devices by JAX's collectives and lax.ppermute only.
A program may use at most 384 MiB of HBM per device.

v0:
```python
import jax
import jax.numpy as jnp
from jax import lax
from jax.sharding import PartitionSpec as P


def slot_waves(owner, slot_count):
    wave_count = owner.shape[0]
    wave_ids = jnp.arange(wave_count, dtype=jnp.int32)
    earlier = (owner[None, :] == owner[:, None]) & (wave_ids[None, :] < wave_ids[:, None])
    ranked = jnp.sum(earlier.astype(jnp.int32), axis=1)
    placed = owner * slot_count + ranked
    matched = placed[None, :] == wave_ids[:, None]
    return jnp.sum(jnp.where(matched, wave_ids[None, :], 0), axis=1)


def block_product(tile_part, source_part):
    return lax.dot_general(
        tile_part, source_part, (((0,), (0,)), ((), ())), preferred_element_type=jnp.float32
    )


def block_zeros(tile_part, source_part):
    return jnp.zeros((tile_part.shape[1], source_part.shape[1]), jnp.float32)


def project_slot(operands):
    table_part, even_rows, odd_rows, counts = operands
    half_rows = table_part.shape[2]
    results = []
    for parity in range(2):
        source = even_rows if parity == 0 else odd_rows
        blocks = []
        for block_low in range(0, half_rows, 128):
            block_high = min(block_low + 128, half_rows)
            tile_part = table_part[parity, :, block_low:block_high]
            blocks.append(
                lax.cond(counts[parity] > block_low, block_product, block_zeros, tile_part, source)
            )
        results.append(jnp.concatenate(blocks, axis=0))
    return jnp.stack(results)


def body(fourier, legendre, owner):
    lat_count = lax.axis_size("lat")
    row_count, wave_count, column_count = fourier.shape
    slot_count = wave_count // lat_count
    north_count = row_count * lat_count // 2
    wave_of = slot_waves(owner, slot_count)
    own_waves = lax.dynamic_slice_in_dim(wave_of, lax.axis_index("lat") * slot_count, slot_count)
    parities = jnp.arange(2, dtype=jnp.int32)
    live_count = (wave_count - own_waves[:, None] - parities[None, :] + 1) // 2
    outgoing = jnp.swapaxes(jnp.take(fourier, wave_of, axis=1), 0, 1)
    arrived = lax.all_to_all(outgoing, "lat", split_axis=0, concat_axis=1, tiled=True)
    upper_rows = arrived[:, :north_count].astype(jnp.float32)
    lower_rows = arrived[:, north_count:].astype(jnp.float32)
    even_part = (upper_rows + lower_rows).astype(jnp.bfloat16)
    odd_part = (upper_rows - lower_rows).astype(jnp.bfloat16)
    half_rows = legendre.shape[3]
    initial = jnp.zeros((slot_count, 2, half_rows, column_count), jnp.float32)
    totals = initial + lax.map(
        project_slot,
        (lax.all_gather(legendre, "lev", axis=2, tiled=True), even_part, odd_part, live_count),
    )
    degree = jnp.arange(half_rows, dtype=jnp.int32)
    kept_mask = degree[None, None, :] < live_count[:, :, None]
    return jnp.where(kept_mask[..., None], totals, 0.0).astype(jnp.bfloat16)


def solution(mesh):
    placed = (P("lat", None, "lev"), P("lat", None, "lev", None), P())
    return jax.shard_map(
        body, mesh=mesh, in_specs=placed, out_specs=P("lat", None, None, "lev"), check_vma=False
    )
```

profile of v0, /device:TPU:6, one launch (start us, length us, event | category | flops | bytes accessed | tf_op | source)
XLA Modules:
  0.0 2161.2 jit_solution(2345935885412572591)
XLA Ops:
  9.9 103.4 %gather_fusion = bf16[640,160,256]{2,0,1:T(8,128)(2,1)} fusion(bf16[160,640,256]{2,1,0:T(8,128)(2,1)} %param.17, s32[1024]{0:T(1024)S(1)} %pad_clamp_fusion), kind=kCustom, calls=%fused_computation | custom fusion | bytes 104860160 | tf_op jit(solution)/shard_map/jit(_take)/gather | solution.py:53
  113.3 34.9 %broadcast_select_fusion = bf16[640,160,256]{2,0,1:T(8,128)(2,1)} fusion(bf16[640,160,256]{2,0,1:T(8,128)(2,1)} %gather_fusion, pred[640]{0:T(1024)(128)(4,1)S(1)} %compare_and_fusion), kind=kLoop, calls=%fused_computation.32 | loop fusion | flops 26214400 | bytes 104858240 | tf_op jit(solution)/shard_map/jit(_take)/select_n | solution.py:53
  148.1 47.8 %copy.12 = bf16[640,160,256]{2,1,0:T(8,128)(2,1)} copy(bf16[640,160,256]{2,0,1:T(8,128)(2,1)} %broadcast_select_fusion) | data formatting | bytes 104857600 | tf_op jit(solution)/shard_map/jit(_take)/select_n | solution.py:53
  195.9 9.2 all-to-all-start
  206.2 1125.8 %all-to-all-done = bf16[640,160,256]{2,1,0:T(8,128)(2,1)} async-done(((bf16[640,160,256]{2,1,0:T(8,128)(2,1)}), bf16[640,160,256]{2,1,0:T(8,128)(2,1)}, u32[]{:S(2)}, u32[]{:S(2)}) %all-to-all-start) | async-done | bytes 52428832 | tf_op jit(solution)/shard_map/all_to_all | solution.py:54
  1332.0 34.9 %copy.13 = bf16[80,8,160,256]{3,2,1,0:T(8,128)(2,1)} copy(bf16[80,8,160,256]{3,2,0,1:T(8,128)(2,1)} %bitcast.19) | data formatting | bytes 104857600 | tf_op jit(solution)/shard_map/all_to_all | solution.py:54
  1366.8 35.3 %fusion.20 = (bf16[80,640,256]{2,1,0:T(8,128)(2,1)}, bf16[80,640,256]{2,1,0:T(8,128)(2,1)}) fusion(bf16[80,1280,256]{2,1,0:T(8,128)(2,1)} %bitcast.81), kind=kLoop, calls=%fused_computation.30 | loop fusion | flops 78643200 | bytes 104857600 | tf_op jit(solution)/shard_map/convert_element_type | solution.py:58
  1402.1 733.9 %while.11 = (s32[]{:T(128)}, bf16[80,2,320,256]{3,2,1,0:T(8,128)(2,1)}, s32[80,2]{0,1:T(2,128)S(1)}, bf16[80,2,640,320]{3,2,1,0:T(8,128)(2,1)}, bf16[80,640,256]...) while((s32[]{:T(128)}, ...), condition=%wide.region_15.16_spmd.clone, body=%wide.region_2.15_spmd.sunk.clone | while | flops 211353600 | bytes 7537453 | solution.py:61
  1403.2 1.3 dynamic-slice_bitcast_fusion.7
  1412.9 1.3 dynamic-slice_bitcast_fusion.7
  1422.2 1.3 dynamic-slice_bitcast_fusion.7
  1431.4 1.3 dynamic-slice_bitcast_fusion.7
  1440.7 1.3 dynamic-slice_bitcast_fusion.7
  1449.9 1.3 dynamic-slice_bitcast_fusion.7
  1459.2 1.3 dynamic-slice_bitcast_fusion.7
  1468.4 1.3 dynamic-slice_bitcast_fusion.7
  1477.7 1.3 dynamic-slice_bitcast_fusion.7
  1486.9 1.3 dynamic-slice_bitcast_fusion.7
  1496.2 1.3 dynamic-slice_bitcast_fusion.7
  1505.4 1.3 dynamic-slice_bitcast_fusion.7
  1514.7 1.3 dynamic-slice_bitcast_fusion.7
  1523.9 1.3 dynamic-slice_bitcast_fusion.7
  1533.2 1.3 dynamic-slice_bitcast_fusion.7
  1542.4 1.3 dynamic-slice_bitcast_fusion.7
  1551.7 1.3 dynamic-slice_bitcast_fusion.7
  1560.9 1.3 dynamic-slice_bitcast_fusion.7
  1570.2 1.3 dynamic-slice_bitcast_fusion.7
  1579.4 1.3 dynamic-slice_bitcast_fusion.7
  1588.7 1.3 dynamic-slice_bitcast_fusion.7
  1597.9 1.3 dynamic-slice_bitcast_fusion.7
  1607.2 1.3 dynamic-slice_bitcast_fusion.7
  1616.4 1.3 dynamic-slice_bitcast_fusion.7
  1625.7 1.3 dynamic-slice_bitcast_fusion.7
  1634.9 1.3 dynamic-slice_bitcast_fusion.7
  1644.2 1.3 dynamic-slice_bitcast_fusion.7
  1653.4 1.3 dynamic-slice_bitcast_fusion.7
  1662.7 1.3 dynamic-slice_bitcast_fusion.7
  1671.9 1.3 dynamic-slice_bitcast_fusion.7
  1681.2 1.3 dynamic-slice_bitcast_fusion.7
  1690.4 1.3 dynamic-slice_bitcast_fusion.7
  1699.7 1.3 dynamic-slice_bitcast_fusion.7
  1708.9 1.3 dynamic-slice_bitcast_fusion.7
  1718.1 1.3 dynamic-slice_bitcast_fusion.7
  1727.4 1.3 dynamic-slice_bitcast_fusion.7
  1736.6 1.3 dynamic-slice_bitcast_fusion.7
  1773.6 1.3 dynamic-slice_bitcast_fusion.7
  1782.9 1.3 dynamic-slice_bitcast_fusion.7
  1792.1 1.3 dynamic-slice_bitcast_fusion.7
  1838.4 1.3 dynamic-slice_bitcast_fusion.7
  1856.9 1.3 dynamic-slice_bitcast_fusion.7
  1875.4 1.3 dynamic-slice_bitcast_fusion.7
  1893.9 1.3 dynamic-slice_bitcast_fusion.7
  1912.4 1.3 dynamic-slice_bitcast_fusion.7
  1930.9 1.3 dynamic-slice_bitcast_fusion.7
  1977.1 1.3 dynamic-slice_bitcast_fusion.7
  1986.4 1.3 dynamic-slice_bitcast_fusion.7
  1995.6 1.3 dynamic-slice_bitcast_fusion.7
  2032.1 1.3 dynamic-slice_bitcast_fusion.7
  2040.9 1.3 dynamic-slice_bitcast_fusion.7
  2075.9 1.3 dynamic-slice_bitcast_fusion.7
  2084.6 1.3 dynamic-slice_bitcast_fusion.7
  2119.7 1.3 dynamic-slice_bitcast_fusion.7
  2128.4 1.3 dynamic-slice_bitcast_fusion.7
  2136.1 18.3 select_convert_fusion
  (1481 shorter events, 401.2 us)
Async XLA Ops:
  6.5 1395.6 %all-gather.2.cloned.1.call-start = ((), (), s32[]{:S(2)}) async-start(), calls=%async_computation.1 | async-start | bytes 98304000 | tf_op jit(solution)/shard_map/all_gather | solution.py:63
  9.3 0.6 copy-start
  195.9 1136.0 %all-to-all-start = ((bf16[640,160,256]{2,1,0:T(8,128)(2,1)}), bf16[640,160,256]{2,1,0:T(8,128)(2,1)}, u32[]{:S(2)}, u32[]{:S(2)}) async-start(bf16[640,160,256]{2,1,0:T(8,128)(2,1)} %copy.12), calls=%async_computation | async-start | bytes 104857600 | tf_op jit(solution)/shard_map/all_to_all | solution.py:54
Sparse Core Ops, SparseCore 0:
  8.9 459.1 all-gather.1
where the time goes:
time: 2200 us; the launch traced here: 2160 us
  waiting for transfers between devices  1130 us (51%)
  local copies, waits for them, and re-layouts  436 us (20%)
  loops' own time  349 us (16%)
  other arithmetic  154 us (7%)
  matrix products  73.6 us (3%)
    all_to_all x1, waiting for transfers between devices, body(): lax.all_to_all(outgoing, 'lat', split_axis=0, concat_axis=1, tiled=True)  1130 us
    another operation x1, loops' own time, body(): lax.map(project_slot, (lax.all_gather(legendre, 'lev', axis=2, tiled=True...  340 us
    squeeze x160, local copies, waits for them, and re-layouts, body(): lax.map(project_slot, (lax.all_gather(legendre, 'lev', axis=2, tiled=True...  194 us
    gather x1, local copies, waits for them, and re-layouts, body(): outgoing = jnp.swapaxes(jnp.take(fourier, wave_of, axis=1), 0, 1)  103 us
    dot_general x296, matrix products, block_product(): lax.dot_general(tile_part, source_part, (((0,), (0,)), ((), ())), preferr...  73.6 us
    dynamic_update_slice x80, other arithmetic, body(): lax.map(project_slot, (lax.all_gather(legendre, 'lev', axis=2, tiled=True...  60.2 us
    slice x80, local copies, waits for them, and re-layouts, project_slot(): counts[parity] > block_low  48 us
    select_n x1, local copies, waits for them, and re-layouts, body(): outgoing = jnp.swapaxes(jnp.take(fourier, wave_of, axis=1), 0, 1)  47.8 us
  transfers between devices with their start and end apart: 2, of which 1 were waited for; matrix products, arithmetic and copies ran while one was open for 12% of the time, Pallas kernels for 0%

commit v1 on v0

v1 whole, which is shorter than its diff:
```python
import functools

import jax
import jax.numpy as jnp
from jax import lax
from jax.experimental import pallas as pl
from jax.experimental.pallas import tpu as pltpu
from jax.sharding import PartitionSpec as P

CHUNK_ENDS = (5, 22, 74, 80)
PICK_GROUP = 4
DEGREE_BLOCK = 128


def slot_waves(owner, slot_count):
    wave_count = owner.shape[0]
    wave_ids = jnp.arange(wave_count, dtype=jnp.int32)
    earlier = (owner[None, :] == owner[:, None]) & (wave_ids[None, :] < wave_ids[:, None])
    ranked = jnp.sum(earlier.astype(jnp.int32), axis=1)
    placed = owner * slot_count + ranked
    matched = placed[None, :] == wave_ids[:, None]
    return jnp.sum(jnp.where(matched, wave_ids[None, :], 0), axis=1)


def chunk_bounds(slot_count):
    ends = {slot_count * end // CHUNK_ENDS[-1] for end in CHUNK_ENDS}
    return sorted(ends | {0})


def pick(wave_ref, *refs):
    out_ref = refs[-1]
    for place, source_ref in enumerate(refs[:-1]):
        out_ref[0, place] = source_ref[0]


def pick_chunk(by_owner, turned, low, high):
    _, rows, columns = turned.shape
    lat_count = by_owner.shape[0]
    chunk = high - low
    group = min(chunk, PICK_GROUP)
    last_wave = by_owner.shape[1] - 1

    def source_of(place):
        def place_of(owner, step, wave_ref):
            slot = jnp.minimum(low + step * group + place, last_wave)
            return wave_ref[owner, slot], 0, 0

        return pl.BlockSpec((1, rows, columns), place_of)

    out = jax.ShapeDtypeStruct((lat_count, chunk, rows, columns), turned.dtype)
    return pl.pallas_call(
        pick,
        out_shape=out,
        grid_spec=pltpu.PrefetchScalarGridSpec(
            num_scalar_prefetch=1,
            grid=(lat_count, pl.cdiv(chunk, group)),
            in_specs=[source_of(place) for place in range(group)],
            out_specs=pl.BlockSpec((1, group, rows, columns), lambda owner, step, wave: (owner, step, 0, 0)),
        ),
        cost_estimate=pl.CostEstimate(flops=0, transcendentals=0, bytes_accessed=4 * out.size),
    )(by_owner, *[turned] * group)


def project(first_slot, counts_ref, source_ref, *rest):
    groups, _, rows, columns = source_ref.shape
    half_groups = groups // 2
    table_refs = rest[:half_groups]
    out_ref = rest[-1]
    _, _, _, degrees = table_refs[0].shape
    slot = first_slot + pl.program_id(0)
    upper, lower = [], []
    for place in range(half_groups):
        block = counts_ref[counts_ref.shape[0] - 1, place]
        upper.append(source_ref[block, 0].astype(jnp.float32))
        lower.append(source_ref[half_groups + block, 0].astype(jnp.float32))
    for parity in range(2):
        pairs = zip(upper, lower)
        parts = [north + south if parity == 0 else north - south for north, south in pairs]
        source = jnp.concatenate([part.astype(jnp.bfloat16) for part in parts], axis=0)
        live = counts_ref[slot, parity]
        for low in range(0, degrees, DEGREE_BLOCK):
            high = min(low + DEGREE_BLOCK, degrees)

            @pl.when(live > low)
            def _(low=low, high=high, source=source, live=live, parity=parity):
                tile = jnp.concatenate([ref[0, parity, :, low:high] for ref in table_refs], axis=0)
                total = lax.dot_general(
                    tile, source, (((0,), (0,)), ((), ())), preferred_element_type=jnp.float32
                )
                degree = low + lax.broadcasted_iota(jnp.int32, total.shape, 0)
                out_ref[0, parity, low:high, :] = jnp.where(degree < live, total, 0.0).astype(out_ref.dtype)

            @pl.when(live <= low)
            def _(low=low, high=high, parity=parity):
                out_ref[0, parity, low:high, :] = jnp.zeros((high - low, columns), out_ref.dtype)


def project_chunk(counts, arrived, tables, spectral, first_slot):
    groups, chunk, rows, columns = arrived.shape
    slot_count, parities, table_rows, degrees = tables[0].shape
    in_specs = [pl.BlockSpec((groups, 1, rows, columns), lambda i, counts: (0, i, 0, 0))]
    for _ in tables:
        in_specs.append(
            pl.BlockSpec((1, parities, table_rows, degrees), lambda i, counts: (first_slot + i, 0, 0, 0))
        )
    operands = [counts, arrived, *tables]
    aliases = {}
    if spectral is not None:
        in_specs.append(pl.BlockSpec(memory_space=pl.ANY))
        aliases = {len(operands): 0}
        operands.append(spectral)
    flops = 2 * chunk * parities * len(tables) * table_rows * degrees * columns
    return pl.pallas_call(
        functools.partial(project, first_slot),
        out_shape=jax.ShapeDtypeStruct((slot_count, parities, degrees, columns), jnp.bfloat16),
        grid_spec=pltpu.PrefetchScalarGridSpec(
            num_scalar_prefetch=1,
            grid=(chunk,),
            in_specs=in_specs,
            out_specs=pl.BlockSpec(
                (1, parities, degrees, columns), lambda i, counts: (first_slot + i, 0, 0, 0)
            ),
        ),
        input_output_aliases=aliases,
        cost_estimate=pl.CostEstimate(flops=flops, transcendentals=0, bytes_accessed=4 * arrived.size),
    )(*operands)


def partner(values, distance, count):
    return lax.ppermute(values, "lev", [(place, place ^ distance) for place in range(count)])


def gather_table(legendre, count):
    tables = [legendre]
    distance = count // 2
    while distance:
        tables += [partner(table, distance, count) for table in tables]
        distance //= 2
    offsets = [0]
    distance = count // 2
    while distance:
        offsets += [offset ^ distance for offset in offsets]
        distance //= 2
    return tables, [lax.axis_index("lev") ^ offset for offset in offsets]


def body(fourier, legendre, owner):
    lat_count = lax.axis_size("lat")
    lev_count = lax.axis_size("lev")
    row_count, wave_count, column_count = fourier.shape
    slot_count = wave_count // lat_count
    table_rows = legendre.shape[2]
    wave_of = slot_waves(owner, slot_count)
    by_owner = wave_of.reshape(lat_count, slot_count)
    bounds = chunk_bounds(slot_count)
    chunks = list(zip(bounds[:-1], bounds[1:]))
    turned = None
    arrivals = []
    spectral = None
    done = 0

    def project_next(done, spectral):
        return project_chunk(counts, arrivals[done], tables, spectral, chunks[done][0])

    for index, (low, high) in enumerate(chunks):
        if index == 0:
            waves = by_owner[:, low:high].reshape(-1)
            taken = fourier.at[:, waves, :].get(mode="promise_in_bounds")
            outgoing = jnp.swapaxes(taken, 0, 1).reshape(lat_count, high - low, row_count, column_count)
            outgoing, source, table = lax.optimization_barrier((outgoing, fourier, legendre))
            turned = jnp.swapaxes(source, 0, 1)
            tables, blocks = gather_table(table, lev_count)
            own_waves = lax.dynamic_slice_in_dim(wave_of, lax.axis_index("lat") * slot_count, slot_count)
            parities = jnp.arange(2, dtype=jnp.int32)
            live_count = (wave_count - own_waves[:, None] - parities[None, :] + 1) // 2
            width = max(2, lev_count)
            counts = jnp.zeros((slot_count + 1, width), jnp.int32)
            counts = counts.at[:slot_count, :2].set(live_count)
            counts = counts.at[slot_count, :lev_count].set(jnp.stack(blocks))
        else:
            outgoing = pick_chunk(by_owner, turned, low, high)
        if index == len(chunks) - 1:
            while done < index - 1:
                spectral = project_next(done, spectral)
                done += 1
            if done:
                outgoing, spectral = lax.optimization_barrier((outgoing, spectral))
        arrived = lax.all_to_all(outgoing, "lat", split_axis=0, concat_axis=0, tiled=True)
        if row_count != table_rows:
            arrived = jnp.swapaxes(arrived, 0, 1).reshape(high - low, -1, table_rows, column_count)
            arrived = jnp.swapaxes(arrived, 0, 1)
        arrivals.append(arrived)
    while done < len(chunks):
        spectral = project_next(done, spectral)
        done += 1
    return spectral


def solution(mesh):
    placed = (P("lat", None, "lev"), P("lat", None, "lev", None), P())
    return jax.shard_map(
        body, mesh=mesh, in_specs=placed, out_specs=P("lat", None, None, "lev"), check_vma=False
    )
```

time: 2200 us -> 1200 us (0.55); the launches traced: 2160 us -> 1190 us
  local copies, waits for them, and re-layouts: 436 us -> 64.2 us
  loops' own time: 349 us -> 0 us
  waiting for transfers between devices: 1130 us -> 874 us
  Pallas kernels: 0 us -> 220 us
  other arithmetic: 154 us -> 2.94 us
  matrix products: 73.6 us -> 0 us
    all_to_all x1 -> x4, waiting for transfers between devices: 1130 us -> 435 us  [body(): lax.all_to_all(outgoing, 'lat', split_axis=0, concat_axis=0, tiled=True)]
    ppermute x0 -> x3, waiting for transfers between devices: none -> 439 us  [partner(): lax.ppermute(values, 'lev', [(place, place ^ distance) for place in range...]
    another operation x481 -> x0, loops' own time: 349 us -> none  [the longest x1 340 us: body(): lax.map(project_slot, (lax.all_gather(legendre, 'lev', axis=2, tiled=True...]
    pallas_call x0 -> x7, Pallas kernels: none -> 220 us  [the longest x4 118 us: project_chunk(): pl.pallas_call(functools.partial(project, first_slot), out_shape=jax.Shap...]
    squeeze x160 -> x0, local copies, waits for them, and re-layouts: 194 us -> none  [body(): lax.map(project_slot, (lax.all_gather(legendre, 'lev', axis=2, tiled=True...]
    gather x1 -> x2, local copies, waits for them, and re-layouts: 103 us -> 14.2 us  [body(): taken = fourier.at[:, waves, :].get(mode='promise_in_bounds')]
    dot_general x296 -> x0, matrix products: 73.6 us -> none  [block_product(): lax.dot_general(tile_part, source_part, (((0,), (0,)), ((), ())), preferr...]
    dynamic_update_slice x80 -> x0, other arithmetic: 60.2 us -> none  [body(): lax.map(project_slot, (lax.all_gather(legendre, 'lev', axis=2, tiled=True...]
  transfers between devices with their start and end apart: 2 -> 7, of which waited for: 1 -> 5; matrix products, arithmetic and copies ran while one was open for 12% -> 4% of each run, Pallas kernels for 0% -> 18%
where the time goes in v1:
time: 1200 us; the launch traced here: 1190 us
  waiting for transfers between devices  874 us (73%)
  Pallas kernels  220 us (18%)
  local copies, waits for them, and re-layouts  64.2 us (5%)
  starting transfers between devices  25.4 us (2%)
    ppermute x3, waiting for transfers between devices, partner(): lax.ppermute(values, 'lev', [(place, place ^ distance) for place in range...  439 us
    all_to_all x4, waiting for transfers between devices, body(): lax.all_to_all(outgoing, 'lat', split_axis=0, concat_axis=0, tiled=True)  435 us
    pallas_call x4, Pallas kernels, project_chunk(): pl.pallas_call(functools.partial(project, first_slot), out_shape=jax.Shap...  118 us
    pallas_call x3, Pallas kernels, pick_chunk(): pl.pallas_call(pick, out_shape=out, grid_spec=pltpu.PrefetchScalarGridSpe...  102 us
    optimization_barrier x1, local copies, waits for them, and re-layouts, body(): lax.optimization_barrier((outgoing, fourier, legendre))  47.5 us
    all_to_all x4, starting transfers between devices, body(): lax.all_to_all(outgoing, 'lat', split_axis=0, concat_axis=0, tiled=True)  24.9 us
  transfers between devices with their start and end apart: 7, of which 5 were waited for; matrix products, arithmetic and copies ran while one was open for 4% of the time, Pallas kernels for 18%

profile of v1, /device:TPU:6, one launch (start us, length us, event | category | flops | bytes accessed | tf_op | source)
XLA Modules:
  0.0 1186.8 jit_solution(2904019798401309302)
XLA Ops:
  0.0 1.1 convert_reduce_fusion
  1.1 0.7 multiply_add_fusion
  1.8 0.2 select_reduce_fusion
  2.0 0.0 copy-start.3
  2.0 0.1 reshape.99.wave_ref
  2.1 0.0 copy-start.2
  2.1 0.1 reshape.100
  2.2 0.4 copy-done.3
  2.6 11.7 gather_fusion
  14.3 0.0 copy-done.2
  14.3 2.5 copy.11
  16.8 6.3 all-to-all-start.1
  23.2 47.5 %copy.14 = bf16[160,640,256]{2,0,1:T(8,128)(2,1)} copy(bf16[160,640,256]{2,1,0:T(8,128)(2,1)} %param.7) | data formatting | bytes 104857600 | tf_op jit(solution)/shard_map/optimization_barrier | solution.py:170
  70.6 25.8 %shard_map.38 = bf16[8,17,160,256]{3,2,1,0:T(8,128)(2,1)} custom-call(s32[8,80]{1,0:T(8,128)} %copy-done.2, bf16[640,160,256]{2,1,0:T(8,128)(2,1)} %bitcast.13, bf16[640,160,256]{2,1,0:T(8,128)(2,1)} %bitcast.14, bf16[640,160,256]{2,1,0:T(8,128)(2,1)} %bitcast.15, bf16[640,160,256]{2,1,0:T(8,128)(2,1)} %bitcast.16), custom_call_target="tpu_custom_call" | custom-call | bytes 22282240 | tf_op jit(solution)/shard_map/pallas_call | solution.py:51
  96.5 0.0 all-to-all-done.1.source_ref
  96.5 0.0 copy-start
  96.5 1.7 copy-done
  98.2 6.0 all-to-all-start
  104.2 64.3 %shard_map.41 = bf16[8,52,160,256]{3,2,1,0:T(8,128)(2,1)} custom-call(s32[8,80]{1,0:T(8,128)} %copy-done.2, bf16[640,160,256]{2,1,0:T(8,128)(2,1)} %bitcast.17, bf16[640,160,256]{2,1,0:T(8,128)(2,1)} %bitcast.18, bf16[640,160,256]{2,1,0:T(8,128)(2,1)} %bitcast.19, bf16[640,160,256]{2,1,0:T(8,128)(2,1)} %bitcast.20), custom_call_target="tpu_custom_call" | custom-call | bytes 68157440 | tf_op jit(solution)/shard_map/pallas_call | solution.py:51
  168.6 176.7 %all-to-all-done.source_ref = bf16[8,17,160,256]{3,2,1,0:T(8,128)(2,1)} async-done(((bf16[8,17,160,256]{3,2,1,0:T(8,128)(2,1)}), bf16[8,17,160,256]{3,2,1,0:T(8,128)(2,1)}, u32[]{:S(2)}, u32[]{:S(2)}) %all-to-all-start) | async-done | bytes 11141152 | tf_op jit(solution)/shard_map/all_to_all | solution.py:188
  345.2 7.6 all-to-all-start.3
  352.8 0.5 collective-permute-start
  353.3 0.0 collective-permute-start.1
  353.3 422.5 %collective-permute-done.rest_1_ = bf16[80,2,160,320]{3,2,1,0:T(8,128)(2,1)} collective-permute-done((bf16[80,2,160,320]{3,2,1,0:T(8,128)(2,1)}, bf16[80,2,160,320]{3,2,1,0:T(8,128)(2,1)}, u32[]{:S(2)}, u32[]{:S(2)}) %collective-permute-start) | collective-permute-done | bytes 16384032 | tf_op jit(solution)/shard_map/ppermute | solution.py:130
  775.8 0.0 collective-permute-start.2
  775.8 11.5 shard_map.37
  787.4 0.8 dynamic-slice_subtract_fusion
  788.1 0.1 add_select_fusion
  788.2 0.1 add_bitcast_fusion
  788.3 0.2 scatter.9.counts_ref
  788.5 0.0 copy-start.1
  788.5 0.0 collective-permute-done.1.rest_2_
  788.5 16.9 %collective-permute-done.2.rest_3_ = bf16[80,2,160,320]{3,2,1,0:T(8,128)(2,1)} collective-permute-done((bf16[80,2,160,320]{3,2,1,0:T(8,128)(2,1)}, bf16[80,2,160,320]{3,2,1,0:T(8,128)(2,1)}, u32[]{:S(2)}, u32[]{:S(2)}) %collective-permute-start.2) | collective-permute-done | bytes 16384032 | tf_op jit(solution)/shard_map/ppermute | solution.py:130
  805.4 0.0 copy-done.1
  805.4 10.4 shard_map.39.rest_4_
  815.9 27.4 %shard_map.40.rest_4_ = bf16[80,2,320,256]{3,2,1,0:T(8,128)(2,1)} custom-call(s32[81,4]{1,0:T(8,128)} %copy-done.1, bf16[8,17,160,256]{3,2,1,0:T(8,128)(2,1)} %all-to-all-done.source_ref, bf16[80,2,160,320]{3,2,1,0:T(8,128)(2,1)} %rest_0_.3, bf16[80,2,160,320]{3,2,1,0:T(8,128)(2,1)} %collective-permute-done.rest_1_, ...), custom_call_target="tpu_custom_call", output_to_operand_aliasing={{}: (6, {})} | custom-call | flops 3565158400 | bytes 22282240 | tf_op jit(solution)/shard_map/pallas_call | solution.py:113
  843.2 241.4 %all-to-all-done.3.source_ref = bf16[8,52,160,256]{3,2,1,0:T(8,128)(2,1)} async-done(((bf16[8,52,160,256]{3,2,1,0:T(8,128)(2,1)}), bf16[8,52,160,256]{3,2,1,0:T(8,128)(2,1)}, u32[]{:S(2)}, u32[]{:S(2)}) %all-to-all-start.3) | async-done | bytes 34078752 | tf_op jit(solution)/shard_map/all_to_all | solution.py:188
  1084.6 5.0 all-to-all-start.2
  1089.6 70.5 %shard_map.42.rest_4_ = bf16[80,2,320,256]{3,2,1,0:T(8,128)(2,1)} custom-call(s32[81,4]{1,0:T(8,128)} %copy-done.1, bf16[8,52,160,256]{3,2,1,0:T(8,128)(2,1)} %all-to-all-done.3.source_ref, bf16[80,2,160,320]{3,2,1,0:T(8,128)(2,1)} %rest_0_.3, bf16[80,2,160,320]{3,2,1,0:T(8,128)(2,1)} %collective-permute-done.rest_1_, ...), custom_call_target="tpu_custom_call", output_to_operand_aliasing={{}: (6, {})} | custom-call | flops 10905190400 | bytes 68157440 | tf_op jit(solution)/shard_map/pallas_call | solution.py:113
  1160.1 16.6 %all-to-all-done.2.source_ref = bf16[8,6,160,256]{3,2,1,0:T(8,128)(2,1)} async-done(((bf16[8,6,160,256]{3,2,1,0:T(8,128)(2,1)}), bf16[8,6,160,256]{3,2,1,0:T(8,128)(2,1)}, u32[]{:S(2)}, u32[]{:S(2)}) %all-to-all-start.2) | async-done | bytes 3932192 | tf_op jit(solution)/shard_map/all_to_all | solution.py:188
  1176.7 10.1 shard_map.43
  (3 shorter events, 0.0 us)
Async XLA Ops:
  2.0 0.6 copy-start.3
  2.1 12.2 %copy-start.2 = (s32[8,80]{1,0:T(8,128)}, s32[8,80]{1,0:T(8,128)S(1)}, u32[]{:S(2)}) copy-start(s32[8,80]{1,0:T(8,128)S(1)} %reshape.99.wave_ref) | copy-start | bytes 7684
  16.8 79.6 %all-to-all-start.1 = ((bf16[8,5,160,256]{3,2,1,0:T(8,128)(2,1)}), bf16[8,5,160,256]{3,2,1,0:T(8,128)(2,1)S(1)}, u32[]{:S(2)}, u32[]{:S(2)}) async-start(bf16[8,5,160,256]{3,2,1,0:T(8,128)(2,1)} %bitcast.6), calls=%async_computation.1 | async-start | bytes 6553600 | tf_op jit(solution)/shard_map/all_to_all | solution.py:188
  96.5 1.7 copy-start
  98.2 247.0 %all-to-all-start = ((bf16[8,17,160,256]{3,2,1,0:T(8,128)(2,1)}), bf16[8,17,160,256]{3,2,1,0:T(8,128)(2,1)}, u32[]{:S(2)}, u32[]{:S(2)}) async-start(bf16[8,17,160,256]{3,2,1,0:T(8,128)(2,1)} %shard_map.38), calls=%async_computation | async-start | bytes 22282240 | tf_op jit(solution)/shard_map/all_to_all | solution.py:188
  345.2 739.4 %all-to-all-start.3 = ((bf16[8,52,160,256]{3,2,1,0:T(8,128)(2,1)}), bf16[8,52,160,256]{3,2,1,0:T(8,128)(2,1)}, u32[]{:S(2)}, u32[]{:S(2)}) async-start(bf16[8,52,160,256]{3,2,1,0:T(8,128)(2,1)} %shard_map.41), calls=%async_computation.3 | async-start | bytes 68157440 | tf_op jit(solution)/shard_map/all_to_all | solution.py:188
  352.8 423.0 %collective-permute-start = (bf16[80,2,160,320]{3,2,1,0:T(8,128)(2,1)}, bf16[80,2,160,320]{3,2,1,0:T(8,128)(2,1)}, u32[]{:S(2)}, u32[]{:S(2)}) collective-permute-start(bf16[80,2,160,320]{3,2,1,0:T(8,128)(2,1)} %rest_0_.3), channel_id=1, source_target_pairs={{0,2},{1,3},{2,0},{3,1},{4,6},{5,7},{6,4},{7,5},{8,10},{9,11},{10,... | collective-permute-start | bytes 49152008 | tf_op jit(solution)/shard_map/ppermute | solution.py:130
  353.3 435.2 %collective-permute-start.1 = (bf16[80,2,160,320]{3,2,1,0:T(8,128)(2,1)}, bf16[80,2,160,320]{3,2,1,0:T(8,128)(2,1)}, u32[]{:S(2)}, u32[]{:S(2)}) collective-permute-start(bf16[80,2,160,320]{3,2,1,0:T(8,128)(2,1)} %rest_0_.3), channel_id=1, source_target_pairs={{0,1},{1,0},{2,3},{3,2},{4,5},{5,4},{6,7},{7,6},{8,9},{9,8},{10,11... | collective-permute-start | bytes 49152008 | tf_op jit(solution)/shard_map/ppermute | solution.py:130
  775.8 29.6 %collective-permute-start.2 = (bf16[80,2,160,320]{3,2,1,0:T(8,128)(2,1)}, bf16[80,2,160,320]{3,2,1,0:T(8,128)(2,1)}, u32[]{:S(2)}, u32[]{:S(2)}) collective-permute-start(bf16[80,2,160,320]{3,2,1,0:T(8,128)(2,1)} %collective-permute-done.rest_1_), channel_id=1, source_target_pairs={{0,1},{1,0},{2,3},{3,2},{4,5},{5,4},{6,7},{7,6},{8,9},{9,8},{10,11... | collective-permute-start | bytes 49152008 | tf_op jit(solution)/shard_map/ppermute | solution.py:130
  788.5 16.9 %copy-start.1 = (s32[81,4]{1,0:T(8,128)}, s32[81,4]{1,0:T(8,128)S(1)}, u32[]{:S(2)}) copy-start(s32[81,4]{1,0:T(8,128)S(1)} %scatter.9.counts_ref) | copy-start | bytes 3892
  1084.6 92.1 %all-to-all-start.2 = ((bf16[8,6,160,256]{3,2,1,0:T(8,128)(2,1)}), bf16[8,6,160,256]{3,2,1,0:T(8,128)(2,1)}, u32[]{:S(2)}, u32[]{:S(2)}) async-start(bf16[8,6,160,256]{3,2,1,0:T(8,128)(2,1)} %shard_map.37), calls=%async_computation.2 | async-start | bytes 7864320 | tf_op jit(solution)/shard_map/all_to_all | solution.py:188

commit v2 on v1

--- a/solution.py
+++ b/solution.py
@@ -7,7 +7,10 @@
 from jax.experimental.pallas import tpu as pltpu
 from jax.sharding import PartitionSpec as P
 
+
 CHUNK_ENDS = (5, 22, 74, 80)
+SWAP_ENDS = (4, 12, 58, 74, 78, 80)
+PROJECT_GROUP = 2
 PICK_GROUP = 4
 DEGREE_BLOCK = 128
 
@@ -22,8 +25,8 @@
     return jnp.sum(jnp.where(matched, wave_ids[None, :], 0), axis=1)
 
 
-def chunk_bounds(slot_count):
-    ends = {slot_count * end // CHUNK_ENDS[-1] for end in CHUNK_ENDS}
+def chunk_bounds(slot_count, chunk_ends=CHUNK_ENDS):
+    ends = {slot_count * end // chunk_ends[-1] for end in chunk_ends}
     return sorted(ends | {0})
 
 
@@ -62,7 +65,7 @@
 
 
 def project(first_slot, counts_ref, source_ref, *rest):
-    groups, _, rows, columns = source_ref.shape
+    groups, _, _, columns = source_ref.shape
     half_groups = groups // 2
     table_refs = rest[:half_groups]
     out_ref = rest[-1]
@@ -144,7 +147,7 @@
     return tables, [lax.axis_index("lev") ^ offset for offset in offsets]
 
 
-def body(fourier, legendre, owner):
+def exchange_body(fourier, legendre, owner):
     lat_count = lax.axis_size("lat")
     lev_count = lax.axis_size("lev")
     row_count, wave_count, column_count = fourier.shape
@@ -196,6 +199,192 @@
     return spectral
 
 
+def pick_each(wave_ref, *refs):
+    count = len(refs) // 2
+    for source_ref, out_ref in zip(refs[:count], refs[count:]):
+        out_ref[...] = source_ref[...]
+
+
+def pick_swaps(by_peer, turned, low, high):
+    _, rows, columns = turned.shape
+    peers = by_peer.shape[0]
+
+    def source_of(peer):
+        return pl.BlockSpec((1, rows, columns), lambda step, wave_ref: (wave_ref[peer, low + step], 0, 0))
+
+    out = jax.ShapeDtypeStruct((high - low, rows, columns), turned.dtype)
+    return pl.pallas_call(
+        pick_each,
+        out_shape=[out] * peers,
+        grid_spec=pltpu.PrefetchScalarGridSpec(
+            num_scalar_prefetch=1,
+            grid=(high - low,),
+            in_specs=[source_of(peer) for peer in range(peers)],
+            out_specs=[pl.BlockSpec((1, rows, columns), lambda step, wave_ref: (step, 0, 0))] * peers,
+        ),
+        cost_estimate=pl.CostEstimate(flops=0, transcendentals=0, bytes_accessed=4 * peers * out.size),
+    )(by_peer, *[turned] * peers)
+
+
+def stack_blocks(places_ref, *refs):
+    out_ref = refs[-1]
+    _, parities, rows, _ = refs[0].shape
+    for index, table_ref in enumerate(refs[:-1]):
+        first_row = pl.multiple_of(places_ref[index] * rows, rows)
+        for parity in range(parities):
+            out_ref[0, parity, pl.ds(first_row, rows), :] = table_ref[0, parity]
+
+
+def stack_tables(places, tables):
+    slot_count, parities, rows, degrees = tables[0].shape
+    whole = (1, parities, rows * len(tables), degrees)
+    out = jax.ShapeDtypeStruct((slot_count, *whole[1:]), tables[0].dtype)
+    return pl.pallas_call(
+        stack_blocks,
+        out_shape=out,
+        grid_spec=pltpu.PrefetchScalarGridSpec(
+            num_scalar_prefetch=1,
+            grid=(slot_count,),
+            in_specs=[pl.BlockSpec((1, parities, rows, degrees), lambda i, places: (i, 0, 0, 0))] * len(tables),
+            out_specs=pl.BlockSpec(whole, lambda i, places: (i, 0, 0, 0)),
+        ),
+        cost_estimate=pl.CostEstimate(flops=0, transcendentals=0, bytes_accessed=4 * out.size),
+    )(places, *tables)
+
+
+def project_swapped(first_slot, peers, counts_ref, *refs):
+    same_refs = refs[: peers // 2]
+    other_refs = refs[peers // 2 : peers]
+    table_ref = refs[peers]
+    out_ref = refs[-1]
+    group = out_ref.shape[0]
+    sign = counts_ref[counts_ref.shape[0] - 1, 0].astype(jnp.float32).astype(jnp.bfloat16)
+    for place in range(group):
+        slot = first_slot + pl.program_id(0) * group + place
+        same = [ref[place] for ref in same_refs]
+        other = [ref[place] for ref in other_refs]
+        for parity in range(2):
+            if parity == 0:
+                parts = [near + far for near, far in zip(same, other)]
+            else:
+                parts = [(near - far) * sign for near, far in zip(same, other)]
+            total = lax.dot_general(
+                table_ref[place, parity],
+                jnp.concatenate(parts, axis=0),
+                (((0,), (0,)), ((), ())),
+                preferred_element_type=jnp.float32,
+            )
+            degree = lax.broadcasted_iota(jnp.int32, total.shape, 0)
+            kept = jnp.where(degree < counts_ref[slot, parity], total, 0.0)
+            out_ref[place, parity] = kept.astype(out_ref.dtype)
+
+
+def project_swaps(counts, arrived, table, spectral, first_slot):
+    chunk, rows, columns = arrived[0].shape
+    slot_count, parities, table_rows, degrees = table.shape
+    group = PROJECT_GROUP
+    first_group = first_slot // group
+    in_specs = [pl.BlockSpec((group, rows, columns), lambda i, counts: (i, 0, 0)) for _ in arrived]
+    in_specs.append(
+        pl.BlockSpec((group, parities, table_rows, degrees), lambda i, counts: (first_group + i, 0, 0, 0))
+    )
+    operands = [counts, *arrived, table]
+    aliases = {}
+    if spectral is not None:
+        in_specs.append(pl.BlockSpec(memory_space=pl.ANY))
+        aliases = {len(operands): 0}
+        operands.append(spectral)
+    flops = 2 * chunk * parities * table_rows * degrees * columns
+    moved = 2 * chunk * (len(arrived) * rows * columns + parities * degrees * (table_rows + columns))
+    return pl.pallas_call(
+        functools.partial(project_swapped, first_slot, len(arrived)),
+        out_shape=jax.ShapeDtypeStruct((slot_count, parities, degrees, columns), jnp.bfloat16),
+        grid_spec=pltpu.PrefetchScalarGridSpec(
+            num_scalar_prefetch=1,
+            grid=(chunk // group,),
+            in_specs=in_specs,
+            out_specs=pl.BlockSpec(
+                (group, parities, degrees, columns), lambda i, counts: (first_group + i, 0, 0, 0)
+            ),
+        ),
+        input_output_aliases=aliases,
+        cost_estimate=pl.CostEstimate(flops=flops, transcendentals=0, bytes_accessed=moved),
+    )(*operands)
+
+
+def swap_order(peers):
+    return [*range(peers // 2, peers), *range(1, peers // 2)]
+
+
+def swap_body(fourier, legendre, owner):
+    peers = lax.axis_size("lat")
+    lev_count = lax.axis_size("lev")
+    row_count, wave_count, column_count = fourier.shape
+    slot_count = wave_count // peers
+    here = lax.axis_index("lat")
+    wave_of = slot_waves(owner, slot_count)
+    by_peer = jnp.take(
+        wave_of.reshape(peers, slot_count), here ^ jnp.arange(peers), axis=0, mode="clip"
+    )
+    bounds = chunk_bounds(slot_count, SWAP_ENDS)
+    chunks = list(zip(bounds[:-1], bounds[1:]))
+    own_waves = by_peer[0]
+    parities = jnp.arange(2, dtype=jnp.int32)
+    live_count = (wave_count - own_waves[:, None] - parities[None, :] + 1) // 2
+    sign = jnp.where(here < peers // 2, 1, -1).astype(jnp.int32)
+    counts = jnp.concatenate([live_count, jnp.full((1, 2), sign, jnp.int32)], axis=0)
+    arrivals = []
+    spectral = None
+    stacked = None
+    done = 0
+
+    def project_next(done, spectral):
+        return project_swaps(counts, arrivals[done], stacked, spectral, bounds[done])
+
+    for index, (low, high) in enumerate(chunks):
+        if index == 0:
+            waves = by_peer[:, low:high].reshape(-1)
+            taken = fourier.at[:, waves, :].get(mode="promise_in_bounds")
+            taken = jnp.swapaxes(taken, 0, 1).reshape(peers, high - low, row_count, column_count)
+            outgoing = [taken[peer] for peer in range(peers)]
+            *outgoing, source, table = lax.optimization_barrier((*outgoing, fourier, legendre))
+            turned = jnp.swapaxes(source, 0, 1)
+            tables = [table, partner(table, lev_count // 2, lev_count)]
+        else:
+            outgoing = pick_swaps(by_peer, turned, low, high)
+        if index >= 2:
+            settled = arrivals[index - 2]
+            outgoing = list(lax.optimization_barrier((*outgoing, *settled))[:peers])
+        arrived = list(outgoing)
+        for distance in swap_order(peers):
+            pairs = [(place, place ^ distance) for place in range(peers)]
+            arrived[distance] = lax.ppermute(outgoing[distance], "lat", pairs)
+        arrivals.append(arrived)
+    offsets = [0, lev_count // 2]
+    distance = lev_count // 4
+    while distance:
+        tables += [partner(piece, distance, lev_count) for piece in tables]
+        offsets += [offset ^ distance for offset in offsets]
+        distance //= 2
+    base = lax.axis_index("lev") ^ (here % lev_count)
+    stacked = stack_tables(jnp.stack([base ^ offset for offset in offsets]), tables)
+    while done < len(chunks):
+        spectral = project_next(done, spectral)
+        done += 1
+    return spectral
+
+
+def swaps_fit(lat_count, lev_count, fourier_shape, table_shape):
+    paired = lat_count == 2 * lev_count and lev_count == 4
+    return paired and fourier_shape[0] == table_shape[2] and fourier_shape[1] % (lat_count * SWAP_ENDS[-1]) == 0
+
+
+def body(fourier, legendre, owner):
+    if swaps_fit(lax.axis_size("lat"), lax.axis_size("lev"), fourier.shape, legendre.shape):
+        return swap_body(fourier, legendre, owner)
+    return exchange_body(fourier, legendre, owner)
+
+
 def solution(mesh):
     placed = (P("lat", None, "lev"), P("lat", None, "lev", None), P())
     return jax.shard_map(

time: 1200 us -> 1820 us (1.52)
  waiting for transfers between devices: 874 us -> 1410 us
  starting transfers between devices: 25.4 us -> 112 us
    ppermute x0 -> x42, waiting for transfers between devices: none -> 986 us  [swap_body(): arrived[distance] = lax.ppermute(outgoing[distance], 'lat', pairs)]
    all_to_all x4 -> x0, waiting for transfers between devices: 435 us -> none  [body(): lax.all_to_all(outgoing, 'lat', split_axis=0, concat_axis=0, tiled=True)]
    ppermute x0 -> x42, starting transfers between devices: none -> 112 us  [swap_body(): arrived[distance] = lax.ppermute(outgoing[distance], 'lat', pairs)]
    all_to_all x4 -> x0, starting transfers between devices: 24.9 us -> none  [body(): lax.all_to_all(outgoing, 'lat', split_axis=0, concat_axis=0, tiled=True)]
    pallas_call x7 -> x12, Pallas kernels: 220 us -> 231 us  [the longest x6 83.5 us: project_swaps(): pl.pallas_call(functools.partial(project_swapped, first_slot, len(arrived...]
    optimization_barrier x1 -> x9, local copies, waits for them, and re-layouts: 47.5 us -> 48.5 us  [swap_body(): lax.optimization_barrier((*outgoing, fourier, legendre))]
  transfers between devices with their start and end apart: 7 -> 45, of which waited for: 5 -> 13; matrix products, arithmetic and copies ran while one was open for 4% -> 3% of each run, Pallas kernels for 18% -> 12%
where the time goes in v2:
time: 1820 us
  waiting for transfers between devices  1410 us (77%)
  Pallas kernels  231 us (13%)
  starting transfers between devices  112 us (6%)
  local copies, waits for them, and re-layouts  60.3 us (3%)
    ppermute x42, waiting for transfers between devices, swap_body(): arrived[distance] = lax.ppermute(outgoing[distance], 'lat', pairs)  986 us
    ppermute x3, waiting for transfers between devices, partner(): lax.ppermute(values, 'lev', [(place, place ^ distance) for place in range...  424 us
    ppermute x42, starting transfers between devices, swap_body(): arrived[distance] = lax.ppermute(outgoing[distance], 'lat', pairs)  112 us
    pallas_call x6, Pallas kernels, project_swaps(): pl.pallas_call(functools.partial(project_swapped, first_slot, len(arrived...  83.5 us
    pallas_call x1, Pallas kernels, stack_tables(): pl.pallas_call(stack_blocks, out_shape=out, grid_spec=pltpu.PrefetchScala...  82.5 us
    pallas_call x5, Pallas kernels, pick_swaps(): pl.pallas_call(pick_each, out_shape=[out] * peers, grid_spec=pltpu.Prefet...  64.9 us
    optimization_barrier x9, local copies, waits for them, and re-layouts, swap_body(): lax.optimization_barrier((*outgoing, fourier, legendre))  48.5 us
  transfers between devices with their start and end apart: 45, of which 13 were waited for; matrix products, arithmetic and copies ran while one was open for 3% of the time, Pallas kernels for 12%

profile of v2, /device:TPU:6, one launch (start us, length us, event | category | flops | bytes accessed | tf_op | source)
XLA Modules:
  0.0 1816.9 jit_solution(11228310811636901893)
XLA Ops:
  0.0 1.1 convert_reduce_fusion
  1.1 0.7 multiply_add_fusion
  2.8 7.4 gather_fusion.1
  10.1 0.8 fusion.5
  11.3 0.8 copy.28.refs_0_
  12.6 423.6 %collective-permute-done.21.refs_1_ = bf16[80,2,160,320]{3,2,1,0:T(8,128)(2,1)} collective-permute-done((bf16[80,2,160,320]{3,2,1,0:T(8,128)(2,1)}, bf16[80,2,160,320]{3,2,1,0:T(8,128)(2,1)}, u32[]{:S(2)}, u32[]{:S(2)}) %collective-permute-start.21) | collective-permute-done | bytes 16384032 | tf_op jit(solution)/shard_map/ppermute | solution.py:133
  436.7 1.6 collective-permute-start.25
  438.2 1.4 collective-permute-start.26
  439.6 6.7 collective-permute-done.24.refs_1_
  446.4 2.6 collective-permute-start.27
  448.9 1.9 collective-permute-start.28
  450.9 10.8 collective-permute-done.26.refs_3_
  461.6 1.3 collective-permute-start.29
  463.0 16.0 collective-permute-done.27.refs_4_
  479.0 3.6 collective-permute-start.30
  482.6 47.5 %copy.37 = bf16[160,640,256]{2,0,1:T(8,128)(2,1)} copy(bf16[160,640,256]{2,1,0:T(8,128)(2,1)} %param.3) | data formatting | bytes 104857600 | tf_op jit(solution)/shard_map/optimization_barrier | solution.py:350
  530.1 8.1 shard_map.39
  538.2 1.6 collective-permute-start
  539.8 0.7 copy-done.6
  540.5 1.3 collective-permute-start.2
  541.8 12.7 collective-permute-done.refs_1_
  554.5 16.2 collective-permute-done.1.refs_2_
  570.7 2.6 collective-permute-start.4
  573.3 35.0 %shard_map.42 = (bf16[46,160,256]{2,1,0:T(8,128)(2,1)}, bf16[46,160,256]{2,1,0:T(8,128)(2,1)}, bf16[46,160,256]{2,1,0:T(8,128)(2,1)}, bf16[46,160,256]{2,1,0:T(8...) custom-call(s32[8,80]{1,0:T(8,128)} %copy-done.14, ...), custom_call_target="tpu_custom_call" | custom-call | bytes 60293120 | tf_op jit(solution)/shard_map/pallas_call | solution.py:216
  608.8 2.1 collective-permute-start.5
  610.9 26.0 %collective-permute-done.4.refs_5_ = bf16[8,160,256]{2,1,0:T(8,128)(2,1)S(1)} collective-permute-done((bf16[8,160,256]{2,1,0:T(8,128)(2,1)}, bf16[8,160,256]{2,1,0:T(8,128)(2,1)S(1)}, u32[]{:S(2)}, u32[]{:S(2)}) %collective-permute-start.4) | collective-permute-done | bytes 655392 | tf_op jit(solution)/shard_map/ppermute | solution.py:361
  636.9 13.7 shard_map.38
  650.7 2.0 collective-permute-start.7
  652.7 14.4 collective-permute-start.8
  667.1 71.6 %collective-permute-done.7.refs_1_ = bf16[16,160,256]{2,1,0:T(8,128)(2,1)} collective-permute-done((bf16[16,160,256]{2,1,0:T(8,128)(2,1)}, bf16[16,160,256]{2,1,0:T(8,128)(2,1)}, u32[]{:S(2)}, u32[]{:S(2)}) %collective-permute-start.7) | collective-permute-done | bytes 1310752 | tf_op jit(solution)/shard_map/ppermute | solution.py:361
  738.7 87.0 %collective-permute-done.9.refs_3_ = bf16[16,160,256]{2,1,0:T(8,128)(2,1)} collective-permute-done((bf16[16,160,256]{2,1,0:T(8,128)(2,1)}, bf16[16,160,256]{2,1,0:T(8,128)(2,1)}, u32[]{:S(2)}, u32[]{:S(2)}) %collective-permute-start.9) | collective-permute-done | bytes 1310752 | tf_op jit(solution)/shard_map/ppermute | solution.py:361
  825.8 1.9 collective-permute-start.33
  827.7 160.5 %collective-permute-done.32.refs_2_ = bf16[46,160,256]{2,1,0:T(8,128)(2,1)} collective-permute-done((bf16[46,160,256]{2,1,0:T(8,128)(2,1)}, bf16[46,160,256]{2,1,0:T(8,128)(2,1)}, u32[]{:S(2)}, u32[]{:S(2)}) %collective-permute-start.32) | collective-permute-done | bytes 3768352 | tf_op jit(solution)/shard_map/ppermute | solution.py:361
  988.2 63.0 %collective-permute-done.33.refs_3_ = bf16[46,160,256]{2,1,0:T(8,128)(2,1)} collective-permute-done((bf16[46,160,256]{2,1,0:T(8,128)(2,1)}, bf16[46,160,256]{2,1,0:T(8,128)(2,1)}, u32[]{:S(2)}, u32[]{:S(2)}) %collective-permute-start.33) | collective-permute-done | bytes 3768352 | tf_op jit(solution)/shard_map/ppermute | solution.py:361
  1051.2 21.1 %collective-permute-start.36 = (bf16[46,160,256]{2,1,0:T(8,128)(2,1)}, bf16[46,160,256]{2,1,0:T(8,128)(2,1)}, u32[]{:S(2)}, u32[]{:S(2)}) collective-permute-start(bf16[46,160,256]{2,1,0:T(8,128)(2,1)} %get-tuple-element.159), channel_id=1, source_target_pairs={{0,24},{4,28},{8,16},{12,20},{16,8},{20,12},{24,0},{28,4},{1,25},{... | collective-permute-start | bytes 11304968 | tf_op jit(solution)/shard_map/ppermute | solution.py:361
  1072.3 301.5 %collective-permute-done.35.refs_5_ = bf16[46,160,256]{2,1,0:T(8,128)(2,1)} collective-permute-done((bf16[46,160,256]{2,1,0:T(8,128)(2,1)}, bf16[46,160,256]{2,1,0:T(8,128)(2,1)}, u32[]{:S(2)}, u32[]{:S(2)}) %collective-permute-start.35) | collective-permute-done | bytes 3768352 | tf_op jit(solution)/shard_map/ppermute | solution.py:361
  1373.8 4.2 collective-permute-start.13
  1378.0 3.1 shard_map.37
  1381.1 5.1 shard_map.41
  1386.2 0.7 subtract_bitcast_fusion
  1387.0 0.6 concatenate.3.counts_ref
  1387.6 213.9 %collective-permute-done.11.refs_5_ = bf16[16,160,256]{2,1,0:T(8,128)(2,1)} collective-permute-done((bf16[16,160,256]{2,1,0:T(8,128)(2,1)}, bf16[16,160,256]{2,1,0:T(8,128)(2,1)}, u32[]{:S(2)}, u32[]{:S(2)}) %collective-permute-start.11) | collective-permute-done | bytes 1310752 | tf_op jit(solution)/shard_map/ppermute | solution.py:361
  1601.5 14.5 collective-permute-start.39
  1615.9 0.6 pad_add_fusion.places_ref
  1616.6 0.6 collective-permute-start.14
  1617.2 12.9 collective-permute-start.15
  1630.1 1.5 collective-permute-start.40
  1631.6 82.5 %shard_map.40.refs_8_ = bf16[80,2,640,320]{3,2,1,0:T(8,128)(2,1)} custom-call(s32[4]{0:T(128)} %pad_add_fusion.places_ref, bf16[80,2,160,320]{3,2,1,0:T(8,128)(2,1)} %refs_0_, bf16[80,2,160,320]{3,2,1,0:T(8,128)(2,1)} %collective-permute-done.21.refs_1_, bf16[80,2,160,320]{3,2,1,0:T(8,128)(2,1)} %collective-permute-done.22.refs_2_, ...), custom_call_target="tpu_custom_call" | custom-call | bytes 131072000 | tf_op jit(solution)/shard_map/pallas_call | solution.py:242
  1714.1 6.1 shard_map.43.refs_9_
  1720.2 9.5 shard_map.44.refs_9_
  1729.7 3.4 collective-permute-start.41
  1733.2 1.5 collective-permute-start.42
  1734.6 2.5 collective-permute-start.43
  1737.1 1.5 collective-permute-start.44
  1738.6 40.8 %shard_map.45.refs_9_ = bf16[80,2,320,256]{3,2,1,0:T(8,128)(2,1)} custom-call(s32[81,2]{1,0:T(8,128)} %concatenate.3.counts_ref, bf16[46,160,256]{2,1,0:T(8,128)(2,1)} %get-tuple-element.153.refs_0_, bf16[46,160,256]{2,1,0:T(8,128)(2,1)} %collective-permute-done.31.refs_1_, ...), custom_call_target="tpu_custom_call", output_to_operand_aliasing={{}: (10, {})} | custom-call | flops 9646899200 | bytes 82903040 | tf_op jit(solution)/shard_map/pallas_call | solution.py:299
  1779.4 0.6 collective-permute-start.16
  1780.1 3.3 collective-permute-start.17
  1783.4 2.4 collective-permute-start.19
  1785.9 2.4 collective-permute-start.20
  1788.3 15.9 shard_map.46.refs_9_
  1804.2 6.1 shard_map.47.refs_9_
  1810.4 0.6 copy-done.17
  1811.2 0.7 copy-done.21
  1811.8 5.1 shard_map.48
  (119 shorter events, 3.3 us)
Async XLA Ops:
  12.0 424.1 %collective-permute-start.21 = (bf16[80,2,160,320]{3,2,1,0:T(8,128)(2,1)}, bf16[80,2,160,320]{3,2,1,0:T(8,128)(2,1)}, u32[]{:S(2)}, u32[]{:S(2)}) collective-permute-start(bf16[80,2,160,320]{3,2,1,0:T(8,128)(2,1)} %refs_0_), channel_id=1, source_target_pairs={{0,2},{1,3},{2,0},{3,1},{4,6},{5,7},{6,4},{7,5},{8,10},{9,11},{10,... | collective-permute-start | bytes 49152008 | tf_op jit(solution)/shard_map/ppermute | solution.py:133
  12.6 1604.6 %collective-permute-start.22 = (bf16[80,2,160,320]{3,2,1,0:T(8,128)(2,1)}, bf16[80,2,160,320]{3,2,1,0:T(8,128)(2,1)}, u32[]{:S(2)}, u32[]{:S(2)}) collective-permute-start(bf16[80,2,160,320]{3,2,1,0:T(8,128)(2,1)} %refs_0_), channel_id=1, source_target_pairs={{0,1},{1,0},{2,3},{3,2},{4,5},{5,4},{6,7},{7,6},{8,9},{9,8},{10,11... | collective-permute-start | bytes 49152008 | tf_op jit(solution)/shard_map/ppermute | solution.py:133
  436.1 1194.0 %collective-permute-start.23 = (bf16[80,2,160,320]{3,2,1,0:T(8,128)(2,1)}, bf16[80,2,160,320]{3,2,1,0:T(8,128)(2,1)}, u32[]{:S(2)}, u32[]{:S(2)}) collective-permute-start(bf16[80,2,160,320]{3,2,1,0:T(8,128)(2,1)} %collective-permute-done.21.refs_1_), channel_id=1, source_target_pairs={{0,1},{1,0},{2,3},{3,2},{4,5},{5,4},{6,7},{7,6},{8,9},{9,8},{10,11... | collective-permute-start | bytes 49152008 | tf_op jit(solution)/shard_map/ppermute | solution.py:133
  436.1 10.2 collective-permute-start.24
  436.7 12.3 collective-permute-start.25
  438.2 23.4 %collective-permute-start.26 = (bf16[4,160,256]{2,1,0:T(8,128)(2,1)S(1)}, bf16[4,160,256]{2,1,0:T(8,128)(2,1)}, u32[]{:S(2)}, u32[]{:S(2)}) collective-permute-start(bf16[4,160,256]{2,1,0:T(8,128)(2,1)S(1)} %copy.31), channel_id=1, source_target_pairs={{0,12},{4,8},{8,4},{12,0},{16,28},{20,24},{24,20},{28,16},{1,13},{... | collective-permute-start | bytes 983048 | tf_op jit(solution)/shard_map/ppermute | solution.py:361
  446.4 32.7 %collective-permute-start.27 = (bf16[4,160,256]{2,1,0:T(8,128)(2,1)S(1)}, bf16[4,160,256]{2,1,0:T(8,128)(2,1)}, u32[]{:S(2)}, u32[]{:S(2)}) collective-permute-start(bf16[4,160,256]{2,1,0:T(8,128)(2,1)S(1)} %copy.32), channel_id=1, source_target_pairs={{0,16},{4,20},{8,24},{12,28},{16,0},{20,4},{24,8},{28,12},{1,17},{... | collective-permute-start | bytes 983048 | tf_op jit(solution)/shard_map/ppermute | solution.py:361
  448.9 89.2 %collective-permute-start.28 = (bf16[4,160,256]{2,1,0:T(8,128)(2,1)S(1)}, bf16[4,160,256]{2,1,0:T(8,128)(2,1)S(1)}, u32[]{:S(2)}, u32[]{:S(2)}) collective-permute-start(bf16[4,160,256]{2,1,0:T(8,128)(2,1)S(1)} %copy.33), channel_id=1, source_target_pairs={{0,20},{4,16},{8,28},{12,24},{16,4},{20,0},{24,12},{28,8},{1,21},{... | collective-permute-start | bytes 983048 | tf_op jit(solution)/shard_map/ppermute | solution.py:361
  461.6 78.1 %collective-permute-start.29 = (bf16[4,160,256]{2,1,0:T(8,128)(2,1)S(1)}, bf16[4,160,256]{2,1,0:T(8,128)(2,1)S(1)}, u32[]{:S(2)}, u32[]{:S(2)}) collective-permute-start(bf16[4,160,256]{2,1,0:T(8,128)(2,1)S(1)} %copy.34), channel_id=1, source_target_pairs={{0,24},{4,28},{8,16},{12,20},{16,8},{20,12},{24,0},{28,4},{1,25},{... | collective-permute-start | bytes 983048 | tf_op jit(solution)/shard_map/ppermute | solution.py:361
  479.0 60.7 %collective-permute-start.30 = (bf16[4,160,256]{2,1,0:T(8,128)(2,1)S(1)}, bf16[4,160,256]{2,1,0:T(8,128)(2,1)S(1)}, u32[]{:S(2)}, u32[]{:S(2)}) collective-permute-start(bf16[4,160,256]{2,1,0:T(8,128)(2,1)S(1)} %copy.35), channel_id=1, source_target_pairs={{0,28},{4,24},{8,20},{12,16},{16,12},{20,8},{24,4},{28,0},{1,29},{... | collective-permute-start | bytes 983048 | tf_op jit(solution)/shard_map/ppermute | solution.py:361
  538.2 16.3 collective-permute-start
  539.7 31.0 %collective-permute-start.1 = (bf16[8,160,256]{2,1,0:T(8,128)(2,1)}, bf16[8,160,256]{2,1,0:T(8,128)(2,1)}, u32[]{:S(2)}, u32[]{:S(2)}) collective-permute-start(bf16[8,160,256]{2,1,0:T(8,128)(2,1)} %get-tuple-element.106), channel_id=1, source_target_pairs={{0,8},{4,12},{8,0},{12,4},{16,24},{20,28},{24,16},{28,20},{1,9},{5... | collective-permute-start | bytes 1966088 | tf_op jit(solution)/shard_map/ppermute | solution.py:361
  540.5 14.0 copy-start.7
  540.5 67.8 %collective-permute-start.2 = (bf16[8,160,256]{2,1,0:T(8,128)(2,1)}, bf16[8,160,256]{2,1,0:T(8,128)(2,1)S(1)}, u32[]{:S(2)}, u32[]{:S(2)}) collective-permute-start(bf16[8,160,256]{2,1,0:T(8,128)(2,1)} %get-tuple-element.107), channel_id=1, source_target_pairs={{0,12},{4,8},{8,4},{12,0},{16,28},{20,24},{24,20},{28,16},{1,13},{... | collective-permute-start | bytes 1966088 | tf_op jit(solution)/shard_map/ppermute | solution.py:361
  554.5 54.3 %collective-permute-start.3 = (bf16[8,160,256]{2,1,0:T(8,128)(2,1)}, bf16[8,160,256]{2,1,0:T(8,128)(2,1)S(1)}, u32[]{:S(2)}, u32[]{:S(2)}) collective-permute-start(bf16[8,160,256]{2,1,0:T(8,128)(2,1)} %get-tuple-element.108), channel_id=1, source_target_pairs={{0,16},{4,20},{8,24},{12,28},{16,0},{20,4},{24,8},{28,12},{1,17},{... | collective-permute-start | bytes 1966088 | tf_op jit(solution)/shard_map/ppermute | solution.py:361
  570.7 66.2 %collective-permute-start.4 = (bf16[8,160,256]{2,1,0:T(8,128)(2,1)}, bf16[8,160,256]{2,1,0:T(8,128)(2,1)S(1)}, u32[]{:S(2)}, u32[]{:S(2)}) collective-permute-start(bf16[8,160,256]{2,1,0:T(8,128)(2,1)} %get-tuple-element.109), channel_id=1, source_target_pairs={{0,20},{4,16},{8,28},{12,24},{16,4},{20,0},{24,12},{28,8},{1,21},{... | collective-permute-start | bytes 1966088 | tf_op jit(solution)/shard_map/ppermute | solution.py:361
  608.3 42.4 %copy-start = (bf16[8,160,256]{2,1,0:T(8,128)(2,1)}, bf16[8,160,256]{2,1,0:T(8,128)(2,1)S(1)}, u32[]{:S(2)}) copy-start(bf16[8,160,256]{2,1,0:T(8,128)(2,1)S(1)} %collective-permute-done.2.refs_3_) | copy-start | bytes 1966084
  608.3 219.4 %collective-permute-start.31 = (bf16[46,160,256]{2,1,0:T(8,128)(2,1)}, bf16[46,160,256]{2,1,0:T(8,128)(2,1)}, u32[]{:S(2)}, u32[]{:S(2)}) collective-permute-start(bf16[46,160,256]{2,1,0:T(8,128)(2,1)} %get-tuple-element.154), channel_id=1, source_target_pairs={{0,4},{4,0},{8,12},{12,8},{16,20},{20,16},{24,28},{28,24},{1,5},{5... | collective-permute-start | bytes 11304968 | tf_op jit(solution)/shard_map/ppermute | solution.py:361
  608.8 41.9 %copy-start.1 = (bf16[8,160,256]{2,1,0:T(8,128)(2,1)}, bf16[8,160,256]{2,1,0:T(8,128)(2,1)S(1)}, u32[]{:S(2)}) copy-start(bf16[8,160,256]{2,1,0:T(8,128)(2,1)S(1)} %collective-permute-done.3.refs_4_) | copy-start | bytes 1966084
  608.8 41.9 %collective-permute-start.5 = (bf16[8,160,256]{2,1,0:T(8,128)(2,1)}, bf16[8,160,256]{2,1,0:T(8,128)(2,1)S(1)}, u32[]{:S(2)}, u32[]{:S(2)}) collective-permute-start(bf16[8,160,256]{2,1,0:T(8,128)(2,1)} %get-tuple-element.110), channel_id=1, source_target_pairs={{0,24},{4,28},{8,16},{12,20},{16,8},{20,12},{24,0},{28,4},{1,25},{... | collective-permute-start | bytes 1966088 | tf_op jit(solution)/shard_map/ppermute | solution.py:361
  636.9 13.8 copy-start.2
  636.9 13.8 collective-permute-start.6
  650.7 730.4 %copy-start.3 = (bf16[8,160,256]{2,1,0:T(8,128)(2,1)}, bf16[8,160,256]{2,1,0:T(8,128)(2,1)S(1)}, u32[]{:S(2)}) copy-start(bf16[8,160,256]{2,1,0:T(8,128)(2,1)S(1)} %collective-permute-done.5.refs_6_) | copy-start | bytes 1966084
  650.7 730.4 %copy-start.4 = (bf16[8,160,256]{2,1,0:T(8,128)(2,1)}, bf16[8,160,256]{2,1,0:T(8,128)(2,1)S(1)}, u32[]{:S(2)}) copy-start(bf16[8,160,256]{2,1,0:T(8,128)(2,1)S(1)} %collective-permute-done.6.refs_7_) | copy-start | bytes 1966084
  650.7 88.0 %collective-permute-start.7 = (bf16[16,160,256]{2,1,0:T(8,128)(2,1)}, bf16[16,160,256]{2,1,0:T(8,128)(2,1)}, u32[]{:S(2)}, u32[]{:S(2)}) collective-permute-start(bf16[16,160,256]{2,1,0:T(8,128)(2,1)} %get-tuple-element.113), channel_id=1, source_target_pairs={{0,4},{4,0},{8,12},{12,8},{16,20},{20,16},{24,28},{28,24},{1,5},{5... | collective-permute-start | bytes 3932168 | tf_op jit(solution)/shard_map/ppermute | solution.py:361
  652.7 86.0 %collective-permute-start.8 = (bf16[16,160,256]{2,1,0:T(8,128)(2,1)}, bf16[16,160,256]{2,1,0:T(8,128)(2,1)}, u32[]{:S(2)}, u32[]{:S(2)}) collective-permute-start(bf16[16,160,256]{2,1,0:T(8,128)(2,1)} %get-tuple-element.114), channel_id=1, source_target_pairs={{0,8},{4,12},{8,0},{12,4},{16,24},{20,28},{24,16},{28,20},{1,9},{5... | collective-permute-start | bytes 3932168 | tf_op jit(solution)/shard_map/ppermute | solution.py:361
  738.7 87.1 %collective-permute-start.9 = (bf16[16,160,256]{2,1,0:T(8,128)(2,1)}, bf16[16,160,256]{2,1,0:T(8,128)(2,1)}, u32[]{:S(2)}, u32[]{:S(2)}) collective-permute-start(bf16[16,160,256]{2,1,0:T(8,128)(2,1)} %get-tuple-element.115), channel_id=1, source_target_pairs={{0,12},{4,8},{8,4},{12,0},{16,28},{20,24},{24,20},{28,16},{1,13},{... | collective-permute-start | bytes 3932168 | tf_op jit(solution)/shard_map/ppermute | solution.py:361
  738.7 87.1 %collective-permute-start.10 = (bf16[16,160,256]{2,1,0:T(8,128)(2,1)}, bf16[16,160,256]{2,1,0:T(8,128)(2,1)}, u32[]{:S(2)}, u32[]{:S(2)}) collective-permute-start(bf16[16,160,256]{2,1,0:T(8,128)(2,1)} %get-tuple-element.116), channel_id=1, source_target_pairs={{0,16},{4,20},{8,24},{12,28},{16,0},{20,4},{24,8},{28,12},{1,17},{... | collective-permute-start | bytes 3932168 | tf_op jit(solution)/shard_map/ppermute | solution.py:361
  825.7 162.5 %collective-permute-start.32 = (bf16[46,160,256]{2,1,0:T(8,128)(2,1)}, bf16[46,160,256]{2,1,0:T(8,128)(2,1)}, u32[]{:S(2)}, u32[]{:S(2)}) collective-permute-start(bf16[46,160,256]{2,1,0:T(8,128)(2,1)} %get-tuple-element.155), channel_id=1, source_target_pairs={{0,8},{4,12},{8,0},{12,4},{16,24},{20,28},{24,16},{28,20},{1,9},{5... | collective-permute-start | bytes 11304968 | tf_op jit(solution)/shard_map/ppermute | solution.py:361
  825.8 225.5 %collective-permute-start.33 = (bf16[46,160,256]{2,1,0:T(8,128)(2,1)}, bf16[46,160,256]{2,1,0:T(8,128)(2,1)}, u32[]{:S(2)}, u32[]{:S(2)}) collective-permute-start(bf16[46,160,256]{2,1,0:T(8,128)(2,1)} %get-tuple-element.156), channel_id=1, source_target_pairs={{0,12},{4,8},{8,4},{12,0},{16,28},{20,24},{24,20},{28,16},{1,13},{... | collective-permute-start | bytes 11304968 | tf_op jit(solution)/shard_map/ppermute | solution.py:361
  827.7 244.6 %collective-permute-start.34 = (bf16[46,160,256]{2,1,0:T(8,128)(2,1)}, bf16[46,160,256]{2,1,0:T(8,128)(2,1)}, u32[]{:S(2)}, u32[]{:S(2)}) collective-permute-start(bf16[46,160,256]{2,1,0:T(8,128)(2,1)} %get-tuple-element.157), channel_id=1, source_target_pairs={{0,16},{4,20},{8,24},{12,28},{16,0},{20,4},{24,8},{28,12},{1,17},{... | collective-permute-start | bytes 11304968 | tf_op jit(solution)/shard_map/ppermute | solution.py:361
  988.2 385.6 %collective-permute-start.35 = (bf16[46,160,256]{2,1,0:T(8,128)(2,1)}, bf16[46,160,256]{2,1,0:T(8,128)(2,1)}, u32[]{:S(2)}, u32[]{:S(2)}) collective-permute-start(bf16[46,160,256]{2,1,0:T(8,128)(2,1)} %get-tuple-element.158), channel_id=1, source_target_pairs={{0,20},{4,16},{8,28},{12,24},{16,4},{20,0},{24,12},{28,8},{1,21},{... | collective-permute-start | bytes 11304968 | tf_op jit(solution)/shard_map/ppermute | solution.py:361
  1051.2 322.6 %collective-permute-start.36 = (bf16[46,160,256]{2,1,0:T(8,128)(2,1)}, bf16[46,160,256]{2,1,0:T(8,128)(2,1)}, u32[]{:S(2)}, u32[]{:S(2)}) collective-permute-start(bf16[46,160,256]{2,1,0:T(8,128)(2,1)} %get-tuple-element.159), channel_id=1, source_target_pairs={{0,24},{4,28},{8,16},{12,20},{16,8},{20,12},{24,0},{28,4},{1,25},{... | collective-permute-start | bytes 11304968 | tf_op jit(solution)/shard_map/ppermute | solution.py:361
  1072.3 301.5 %collective-permute-start.37 = (bf16[46,160,256]{2,1,0:T(8,128)(2,1)}, bf16[46,160,256]{2,1,0:T(8,128)(2,1)}, u32[]{:S(2)}, u32[]{:S(2)}) collective-permute-start(bf16[46,160,256]{2,1,0:T(8,128)(2,1)} %get-tuple-element.160), channel_id=1, source_target_pairs={{0,28},{4,24},{8,20},{12,16},{16,12},{20,8},{24,4},{28,0},{1,29},{... | collective-permute-start | bytes 11304968 | tf_op jit(solution)/shard_map/ppermute | solution.py:361
  1373.8 227.6 %collective-permute-start.11 = (bf16[16,160,256]{2,1,0:T(8,128)(2,1)}, bf16[16,160,256]{2,1,0:T(8,128)(2,1)}, u32[]{:S(2)}, u32[]{:S(2)}) collective-permute-start(bf16[16,160,256]{2,1,0:T(8,128)(2,1)} %get-tuple-element.117), channel_id=1, source_target_pairs={{0,20},{4,16},{8,28},{12,24},{16,4},{20,0},{24,12},{28,8},{1,21},{... | collective-permute-start | bytes 3932168 | tf_op jit(solution)/shard_map/ppermute | solution.py:361
  1373.8 227.6 %collective-permute-start.12 = (bf16[16,160,256]{2,1,0:T(8,128)(2,1)}, bf16[16,160,256]{2,1,0:T(8,128)(2,1)}, u32[]{:S(2)}, u32[]{:S(2)}) collective-permute-start(bf16[16,160,256]{2,1,0:T(8,128)(2,1)} %get-tuple-element.118), channel_id=1, source_target_pairs={{0,24},{4,28},{8,16},{12,20},{16,8},{20,12},{24,0},{28,4},{1,25},{... | collective-permute-start | bytes 3932168 | tf_op jit(solution)/shard_map/ppermute | solution.py:361
  1373.8 242.7 %collective-permute-start.13 = (bf16[16,160,256]{2,1,0:T(8,128)(2,1)}, bf16[16,160,256]{2,1,0:T(8,128)(2,1)}, u32[]{:S(2)}, u32[]{:S(2)}) collective-permute-start(bf16[16,160,256]{2,1,0:T(8,128)(2,1)} %get-tuple-element.119), channel_id=1, source_target_pairs={{0,28},{4,24},{8,20},{12,16},{16,12},{20,8},{24,4},{28,0},{1,29},{... | collective-permute-start | bytes 3932168 | tf_op jit(solution)/shard_map/ppermute | solution.py:361
  1381.1 235.5 %copy-start.27 = (bf16[2,160,256]{2,1,0:T(8,128)(2,1)S(1)}, bf16[2,160,256]{2,1,0:T(8,128)(2,1)}, u32[]{:S(2)}) copy-start(bf16[2,160,256]{2,1,0:T(8,128)(2,1)} %get-tuple-element.121) | copy-start | bytes 491524
  1381.1 236.1 %copy-start.26 = (bf16[2,160,256]{2,1,0:T(8,128)(2,1)S(1)}, bf16[2,160,256]{2,1,0:T(8,128)(2,1)}, u32[]{:S(2)}) copy-start(bf16[2,160,256]{2,1,0:T(8,128)(2,1)} %get-tuple-element.122) | copy-start | bytes 491524
  1601.5 133.2 %collective-permute-start.38 = (bf16[4,160,256]{2,1,0:T(8,128)(2,1)}, bf16[4,160,256]{2,1,0:T(8,128)(2,1)S(1)}, u32[]{:S(2)}, u32[]{:S(2)}) collective-permute-start(bf16[4,160,256]{2,1,0:T(8,128)(2,1)} %get-tuple-element.162), channel_id=1, source_target_pairs={{0,4},{4,0},{8,12},{12,8},{16,20},{20,16},{24,28},{28,24},{1,5},{5... | collective-permute-start | bytes 983048 | tf_op jit(solution)/shard_map/ppermute | solution.py:361
  1601.5 135.6 %collective-permute-start.39 = (bf16[4,160,256]{2,1,0:T(8,128)(2,1)}, bf16[4,160,256]{2,1,0:T(8,128)(2,1)S(1)}, u32[]{:S(2)}, u32[]{:S(2)}) collective-permute-start(bf16[4,160,256]{2,1,0:T(8,128)(2,1)} %get-tuple-element.163), channel_id=1, source_target_pairs={{0,8},{4,12},{8,0},{12,4},{16,24},{20,28},{24,16},{28,20},{1,9},{5... | collective-permute-start | bytes 983048 | tf_op jit(solution)/shard_map/ppermute | solution.py:361
  1616.6 113.1 %collective-permute-start.14 = (bf16[2,160,256]{2,1,0:T(8,128)(2,1)S(1)}, bf16[2,160,256]{2,1,0:T(8,128)(2,1)S(1)}, u32[]{:S(2)}, u32[]{:S(2)}) collective-permute-start(bf16[2,160,256]{2,1,0:T(8,128)(2,1)S(1)} %copy-done.27), channel_id=1, source_target_pairs={{0,4},{4,0},{8,12},{12,8},{16,20},{20,16},{24,28},{28,24},{1,5},{5... | collective-permute-start | bytes 491528 | tf_op jit(solution)/shard_map/ppermute | solution.py:361
  1617.2 116.0 %collective-permute-start.15 = (bf16[2,160,256]{2,1,0:T(8,128)(2,1)S(1)}, bf16[2,160,256]{2,1,0:T(8,128)(2,1)S(1)}, u32[]{:S(2)}, u32[]{:S(2)}) collective-permute-start(bf16[2,160,256]{2,1,0:T(8,128)(2,1)S(1)} %copy-done.26), channel_id=1, source_target_pairs={{0,8},{4,12},{8,0},{12,4},{16,24},{20,28},{24,16},{28,20},{1,9},{5... | collective-permute-start | bytes 491528 | tf_op jit(solution)/shard_map/ppermute | solution.py:361
  1630.1 149.3 %collective-permute-start.40 = (bf16[4,160,256]{2,1,0:T(8,128)(2,1)}, bf16[4,160,256]{2,1,0:T(8,128)(2,1)}, u32[]{:S(2)}, u32[]{:S(2)}) collective-permute-start(bf16[4,160,256]{2,1,0:T(8,128)(2,1)} %get-tuple-element.164), channel_id=1, source_target_pairs={{0,12},{4,8},{8,4},{12,0},{16,28},{20,24},{24,20},{28,16},{1,13},{... | collective-permute-start | bytes 983048 | tf_op jit(solution)/shard_map/ppermute | solution.py:361
  1720.2 14.5 copy-start.23
  1720.2 16.9 copy-start.22
  1729.7 56.1 %copy-start.25 = (bf16[2,160,256]{2,1,0:T(8,128)(2,1)S(1)}, bf16[2,160,256]{2,1,0:T(8,128)(2,1)}, u32[]{:S(2)}) copy-start(bf16[2,160,256]{2,1,0:T(8,128)(2,1)} %get-tuple-element.127) | copy-start | bytes 491524
  1729.7 49.7 %copy-start.15 = (bf16[2,160,256]{2,1,0:T(8,128)(2,1)}, bf16[2,160,256]{2,1,0:T(8,128)(2,1)S(1)}, u32[]{:S(2)}) copy-start(bf16[2,160,256]{2,1,0:T(8,128)(2,1)S(1)} %collective-permute-done.14.refs_1_) | copy-start | bytes 491524
  1729.7 50.4 %collective-permute-start.41 = (bf16[4,160,256]{2,1,0:T(8,128)(2,1)}, bf16[4,160,256]{2,1,0:T(8,128)(2,1)S(1)}, u32[]{:S(2)}, u32[]{:S(2)}) collective-permute-start(bf16[4,160,256]{2,1,0:T(8,128)(2,1)} %get-tuple-element.165), channel_id=1, source_target_pairs={{0,16},{4,20},{8,24},{12,28},{16,0},{20,4},{24,8},{28,12},{1,17},{... | collective-permute-start | bytes 983048 | tf_op jit(solution)/shard_map/ppermute | solution.py:361
  1733.1 46.3 %copy-start.16 = (bf16[2,160,256]{2,1,0:T(8,128)(2,1)}, bf16[2,160,256]{2,1,0:T(8,128)(2,1)S(1)}, u32[]{:S(2)}) copy-start(bf16[2,160,256]{2,1,0:T(8,128)(2,1)S(1)} %collective-permute-done.15.refs_2_) | copy-start | bytes 491524
  1733.2 50.2 %collective-permute-start.42 = (bf16[4,160,256]{2,1,0:T(8,128)(2,1)S(1)}, bf16[4,160,256]{2,1,0:T(8,128)(2,1)S(1)}, u32[]{:S(2)}, u32[]{:S(2)}) collective-permute-start(bf16[4,160,256]{2,1,0:T(8,128)(2,1)S(1)} %copy-done.24), channel_id=1, source_target_pairs={{0,20},{4,16},{8,28},{12,24},{16,4},{20,0},{24,12},{28,8},{1,21},{... | collective-permute-start | bytes 983048 | tf_op jit(solution)/shard_map/ppermute | solution.py:361
  1734.6 44.8 %copy-start.8 = (bf16[4,160,256]{2,1,0:T(8,128)(2,1)}, bf16[4,160,256]{2,1,0:T(8,128)(2,1)S(1)}, u32[]{:S(2)}) copy-start(bf16[4,160,256]{2,1,0:T(8,128)(2,1)S(1)} %collective-permute-done.38.refs_1_) | copy-start | bytes 983044
  1734.6 48.8 %collective-permute-start.43 = (bf16[4,160,256]{2,1,0:T(8,128)(2,1)S(1)}, bf16[4,160,256]{2,1,0:T(8,128)(2,1)S(1)}, u32[]{:S(2)}, u32[]{:S(2)}) collective-permute-start(bf16[4,160,256]{2,1,0:T(8,128)(2,1)S(1)} %copy-done.23), channel_id=1, source_target_pairs={{0,24},{4,28},{8,16},{12,20},{16,8},{20,12},{24,0},{28,4},{1,25},{... | collective-permute-start | bytes 983048 | tf_op jit(solution)/shard_map/ppermute | solution.py:361
  1737.1 42.3 %copy-start.9 = (bf16[4,160,256]{2,1,0:T(8,128)(2,1)}, bf16[4,160,256]{2,1,0:T(8,128)(2,1)S(1)}, u32[]{:S(2)}) copy-start(bf16[4,160,256]{2,1,0:T(8,128)(2,1)S(1)} %collective-permute-done.39.refs_2_) | copy-start | bytes 983044
  1737.1 48.7 %collective-permute-start.44 = (bf16[4,160,256]{2,1,0:T(8,128)(2,1)S(1)}, bf16[4,160,256]{2,1,0:T(8,128)(2,1)S(1)}, u32[]{:S(2)}, u32[]{:S(2)}) collective-permute-start(bf16[4,160,256]{2,1,0:T(8,128)(2,1)S(1)} %copy-done.22), channel_id=1, source_target_pairs={{0,28},{4,24},{8,20},{12,16},{16,12},{20,8},{24,4},{28,0},{1,29},{... | collective-permute-start | bytes 983048 | tf_op jit(solution)/shard_map/ppermute | solution.py:361
  1779.4 30.8 %collective-permute-start.16 = (bf16[2,160,256]{2,1,0:T(8,128)(2,1)}, bf16[2,160,256]{2,1,0:T(8,128)(2,1)S(1)}, u32[]{:S(2)}, u32[]{:S(2)}) collective-permute-start(bf16[2,160,256]{2,1,0:T(8,128)(2,1)} %get-tuple-element.123), channel_id=1, source_target_pairs={{0,12},{4,8},{8,4},{12,0},{16,28},{20,24},{24,20},{28,16},{1,13},{... | collective-permute-start | bytes 491528 | tf_op jit(solution)/shard_map/ppermute | solution.py:361
  1780.1 24.1 %copy-start.10 = (bf16[4,160,256]{2,1,0:T(8,128)(2,1)}, bf16[4,160,256]{2,1,0:T(8,128)(2,1)S(1)}, u32[]{:S(2)}) copy-start(bf16[4,160,256]{2,1,0:T(8,128)(2,1)S(1)} %collective-permute-done.41.refs_4_) | copy-start | bytes 983044
  1780.1 30.2 %collective-permute-start.17 = (bf16[2,160,256]{2,1,0:T(8,128)(2,1)}, bf16[2,160,256]{2,1,0:T(8,128)(2,1)S(1)}, u32[]{:S(2)}, u32[]{:S(2)}) collective-permute-start(bf16[2,160,256]{2,1,0:T(8,128)(2,1)} %get-tuple-element.124), channel_id=1, source_target_pairs={{0,16},{4,20},{8,24},{12,28},{16,0},{20,4},{24,8},{28,12},{1,17},{... | collective-permute-start | bytes 491528 | tf_op jit(solution)/shard_map/ppermute | solution.py:361
  1783.4 20.8 %copy-start.11 = (bf16[4,160,256]{2,1,0:T(8,128)(2,1)}, bf16[4,160,256]{2,1,0:T(8,128)(2,1)S(1)}, u32[]{:S(2)}) copy-start(bf16[4,160,256]{2,1,0:T(8,128)(2,1)S(1)} %collective-permute-done.42.refs_5_) | copy-start | bytes 983044
  1783.4 26.9 %collective-permute-start.18 = (bf16[2,160,256]{2,1,0:T(8,128)(2,1)}, bf16[2,160,256]{2,1,0:T(8,128)(2,1)S(1)}, u32[]{:S(2)}, u32[]{:S(2)}) collective-permute-start(bf16[2,160,256]{2,1,0:T(8,128)(2,1)} %get-tuple-element.125), channel_id=1, source_target_pairs={{0,20},{4,16},{8,28},{12,24},{16,4},{20,0},{24,12},{28,8},{1,21},{... | collective-permute-start | bytes 491528 | tf_op jit(solution)/shard_map/ppermute | solution.py:361
  1783.4 20.7 %copy-start.12 = (bf16[4,160,256]{2,1,0:T(8,128)(2,1)}, bf16[4,160,256]{2,1,0:T(8,128)(2,1)S(1)}, u32[]{:S(2)}) copy-start(bf16[4,160,256]{2,1,0:T(8,128)(2,1)S(1)} %collective-permute-done.43.refs_6_) | copy-start | bytes 983044
  1783.4 26.9 %collective-permute-start.19 = (bf16[2,160,256]{2,1,0:T(8,128)(2,1)}, bf16[2,160,256]{2,1,0:T(8,128)(2,1)S(1)}, u32[]{:S(2)}, u32[]{:S(2)}) collective-permute-start(bf16[2,160,256]{2,1,0:T(8,128)(2,1)} %get-tuple-element.126), channel_id=1, source_target_pairs={{0,24},{4,28},{8,16},{12,20},{16,8},{20,12},{24,0},{28,4},{1,25},{... | collective-permute-start | bytes 491528 | tf_op jit(solution)/shard_map/ppermute | solution.py:361
  1785.9 18.3 %copy-start.13 = (bf16[4,160,256]{2,1,0:T(8,128)(2,1)}, bf16[4,160,256]{2,1,0:T(8,128)(2,1)S(1)}, u32[]{:S(2)}) copy-start(bf16[4,160,256]{2,1,0:T(8,128)(2,1)S(1)} %collective-permute-done.44.refs_7_) | copy-start | bytes 983044
  1785.9 24.5 %collective-permute-start.20 = (bf16[2,160,256]{2,1,0:T(8,128)(2,1)S(1)}, bf16[2,160,256]{2,1,0:T(8,128)(2,1)S(1)}, u32[]{:S(2)}, u32[]{:S(2)}) collective-permute-start(bf16[2,160,256]{2,1,0:T(8,128)(2,1)S(1)} %copy-done.25), channel_id=1, source_target_pairs={{0,28},{4,24},{8,20},{12,16},{16,12},{20,8},{24,4},{28,0},{1,29},{... | collective-permute-start | bytes 491528 | tf_op jit(solution)/shard_map/ppermute | solution.py:361
  (9 other events, 26.4 us)

commit v3 on v2

--- a/solution.py
+++ b/solution.py
@@ -9,7 +9,7 @@
 
 
 CHUNK_ENDS = (5, 22, 74, 80)
-SWAP_ENDS = (4, 12, 58, 74, 78, 80)
+SWAP_ENDS = (4, 10, 58, 74, 78, 80)
 PROJECT_GROUP = 2
 PICK_GROUP = 4
 DEGREE_BLOCK = 128
@@ -347,7 +347,9 @@
             taken = fourier.at[:, waves, :].get(mode="promise_in_bounds")
             taken = jnp.swapaxes(taken, 0, 1).reshape(peers, high - low, row_count, column_count)
             outgoing = [taken[peer] for peer in range(peers)]
-            *outgoing, source, table = lax.optimization_barrier((*outgoing, fourier, legendre))
+            final = swap_order(peers)[-1]
+            tied = lax.optimization_barrier((outgoing[final], fourier, legendre))
+            outgoing[final], source, table = tied
             turned = jnp.swapaxes(source, 0, 1)
             tables = [table, partner(table, lev_count // 2, lev_count)]
         else:

time: 1820 us -> 1850 us (1.016)
  waiting for transfers between devices: 1410 us -> 1430 us
    ppermute x42, waiting for transfers between devices: 986 us -> 1010 us  [swap_body(): arrived[distance] = lax.ppermute(outgoing[distance], 'lat', pairs)]
    optimization_barrier x9 -> x2, local copies, waits for them, and re-layouts: 48.5 us -> 47.4 us  [swap_body(): tied = lax.optimization_barrier((outgoing[final], fourier, legendre))]
where the time goes in v3:
time: 1850 us; the launch traced here: 1840 us
  waiting for transfers between devices  1430 us (77%)
  Pallas kernels  231 us (12%)
  starting transfers between devices  113 us (6%)
  local copies, waits for them, and re-layouts  63.2 us (3%)
    ppermute x42, waiting for transfers between devices, swap_body(): arrived[distance] = lax.ppermute(outgoing[distance], 'lat', pairs)  1010 us
    ppermute x3, waiting for transfers between devices, partner(): lax.ppermute(values, 'lev', [(place, place ^ distance) for place in range...  424 us
    ppermute x42, starting transfers between devices, swap_body(): arrived[distance] = lax.ppermute(outgoing[distance], 'lat', pairs)  113 us
    pallas_call x6, Pallas kernels, project_swaps(): pl.pallas_call(functools.partial(project_swapped, first_slot, len(arrived...  83.5 us
    pallas_call x1, Pallas kernels, stack_tables(): pl.pallas_call(stack_blocks, out_shape=out, grid_spec=pltpu.PrefetchScala...  82.5 us
    pallas_call x5, Pallas kernels, pick_swaps(): pl.pallas_call(pick_each, out_shape=[out] * peers, grid_spec=pltpu.Prefet...  65.4 us
    optimization_barrier x2, local copies, waits for them, and re-layouts, swap_body(): tied = lax.optimization_barrier((outgoing[final], fourier, legendre))  47.4 us
  transfers between devices with their start and end apart: 45, of which 13 were waited for; matrix products, arithmetic and copies ran while one was open for 3% of the time, Pallas kernels for 12%

profile of v3, /device:TPU:6, one launch (start us, length us, event | category | flops | bytes accessed | tf_op | source)
XLA Modules:
  0.0 1843.9 jit_solution(3808408931389885245)
XLA Ops:
  0.0 1.1 convert_reduce_fusion
  2.8 7.4 gather_fusion.1
  10.1 1.6 fusion.5
  12.3 423.6 %collective-permute-done.21.refs_1_ = bf16[80,2,160,320]{3,2,1,0:T(8,128)(2,1)} collective-permute-done((bf16[80,2,160,320]{3,2,1,0:T(8,128)(2,1)}, bf16[80,2,160,320]{3,2,1,0:T(8,128)(2,1)}, u32[]{:S(2)}, u32[]{:S(2)}) %collective-permute-start.21) | collective-permute-done | bytes 16384032 | tf_op jit(solution)/shard_map/ppermute | solution.py:133
  436.6 1.6 collective-permute-start.25
  438.2 1.4 collective-permute-start.26
  439.6 6.5 collective-permute-done.24.refs_1_
  446.1 2.6 collective-permute-start.27
  448.8 2.0 collective-permute-start.28
  450.8 10.9 collective-permute-done.26.refs_3_
  461.7 1.3 collective-permute-start.29
  463.1 15.6 collective-permute-done.27.refs_4_
  478.7 0.7 copy-done.13
  479.4 3.6 collective-permute-start.30
  483.0 47.4 %copy.37 = bf16[160,640,256]{2,0,1:T(8,128)(2,1)} copy(bf16[160,640,256]{2,1,0:T(8,128)(2,1)} %param.3) | data formatting | bytes 104857600 | tf_op jit(solution)/shard_map/optimization_barrier | solution.py:351
  530.3 6.5 shard_map.39
  536.8 1.6 collective-permute-start
  538.4 0.7 copy-done.15
  539.1 0.7 copy-done.16
  539.9 1.3 collective-permute-start.2
  541.1 8.3 collective-permute-done.refs_1_
  549.5 13.0 collective-permute-done.1.refs_2_
  562.5 0.8 copy-done.4
  563.3 2.6 collective-permute-start.4
  565.8 37.3 %shard_map.42 = (bf16[48,160,256]{2,1,0:T(8,128)(2,1)}, bf16[48,160,256]{2,1,0:T(8,128)(2,1)}, bf16[48,160,256]{2,1,0:T(8,128)(2,1)}, bf16[48,160,256]{2,1,0:T(8...) custom-call(s32[8,80]{1,0:T(8,128)} %copy-done.21, ...), custom_call_target="tpu_custom_call" | custom-call | bytes 62914560 | tf_op jit(solution)/shard_map/pallas_call | solution.py:216
  603.1 0.8 copy.29.refs_0_
  604.3 2.1 collective-permute-start.5
  606.4 2.8 collective-permute-start.6
  609.3 13.6 shard_map.38
  623.5 10.7 collective-permute-start.8
  634.1 79.8 %collective-permute-done.7.refs_1_ = bf16[16,160,256]{2,1,0:T(8,128)(2,1)} collective-permute-done((bf16[16,160,256]{2,1,0:T(8,128)(2,1)}, bf16[16,160,256]{2,1,0:T(8,128)(2,1)}, u32[]{:S(2)}, u32[]{:S(2)}) %collective-permute-start.7) | collective-permute-done | bytes 1310752 | tf_op jit(solution)/shard_map/ppermute | solution.py:363
  713.9 11.5 collective-permute-start.9
  725.4 1.6 collective-permute-start.10
  727.1 86.4 %collective-permute-done.9.refs_3_ = bf16[16,160,256]{2,1,0:T(8,128)(2,1)} collective-permute-done((bf16[16,160,256]{2,1,0:T(8,128)(2,1)}, bf16[16,160,256]{2,1,0:T(8,128)(2,1)}, u32[]{:S(2)}, u32[]{:S(2)}) %collective-permute-start.9) | collective-permute-done | bytes 1310752 | tf_op jit(solution)/shard_map/ppermute | solution.py:363
  813.5 2.8 collective-permute-start.34
  816.2 147.1 %collective-permute-done.32.refs_2_ = bf16[48,160,256]{2,1,0:T(8,128)(2,1)} collective-permute-done((bf16[48,160,256]{2,1,0:T(8,128)(2,1)}, bf16[48,160,256]{2,1,0:T(8,128)(2,1)}, u32[]{:S(2)}, u32[]{:S(2)}) %collective-permute-start.32) | collective-permute-done | bytes 3932192 | tf_op jit(solution)/shard_map/ppermute | solution.py:363
  963.3 2.8 collective-permute-start.35
  966.1 90.9 %collective-permute-done.33.refs_3_ = bf16[48,160,256]{2,1,0:T(8,128)(2,1)} collective-permute-done((bf16[48,160,256]{2,1,0:T(8,128)(2,1)}, bf16[48,160,256]{2,1,0:T(8,128)(2,1)}, u32[]{:S(2)}, u32[]{:S(2)}) %collective-permute-start.33) | collective-permute-done | bytes 3932192 | tf_op jit(solution)/shard_map/ppermute | solution.py:363
  1056.9 10.7 collective-permute-done.34.refs_4_
  1067.7 2.2 collective-permute-start.37
  1069.9 312.9 %collective-permute-done.35.refs_5_ = bf16[48,160,256]{2,1,0:T(8,128)(2,1)} collective-permute-done((bf16[48,160,256]{2,1,0:T(8,128)(2,1)}, bf16[48,160,256]{2,1,0:T(8,128)(2,1)}, u32[]{:S(2)}, u32[]{:S(2)}) %collective-permute-start.35) | collective-permute-done | bytes 3932192 | tf_op jit(solution)/shard_map/ppermute | solution.py:363
  1382.8 5.0 collective-permute-start.12
  1387.8 1.5 collective-permute-start.13
  1389.4 4.9 shard_map.41
  1395.0 226.5 %collective-permute-done.11.refs_5_ = bf16[16,160,256]{2,1,0:T(8,128)(2,1)S(1)} collective-permute-done((bf16[16,160,256]{2,1,0:T(8,128)(2,1)}, bf16[16,160,256]{2,1,0:T(8,128)(2,1)S(1)}, u32[]{:S(2)}, u32[]{:S(2)}) %collective-permute-start.11) | collective-permute-done | bytes 1310752 | tf_op jit(solution)/shard_map/ppermute | solution.py:363
  1621.5 20.1 %collective-permute-start.39 = (bf16[4,160,256]{2,1,0:T(8,128)(2,1)}, bf16[4,160,256]{2,1,0:T(8,128)(2,1)}, u32[]{:S(2)}, u32[]{:S(2)}) collective-permute-start(bf16[4,160,256]{2,1,0:T(8,128)(2,1)} %get-tuple-element.149), channel_id=1, source_target_pairs={{0,8},{4,12},{8,0},{12,4},{16,24},{20,28},{24,16},{28,20},{1,9},{5... | collective-permute-start | bytes 983048 | tf_op jit(solution)/shard_map/ppermute | solution.py:363
  1641.7 3.1 shard_map.37
  1646.9 12.5 collective-permute-start.15
  1659.4 82.5 %shard_map.40.refs_8_ = bf16[80,2,640,320]{3,2,1,0:T(8,128)(2,1)} custom-call(s32[4]{0:T(128)} %pad_add_fusion.places_ref, bf16[80,2,160,320]{3,2,1,0:T(8,128)(2,1)} %refs_0_, bf16[80,2,160,320]{3,2,1,0:T(8,128)(2,1)} %collective-permute-done.21.refs_1_, bf16[80,2,160,320]{3,2,1,0:T(8,128)(2,1)} %collective-permute-done.22.refs_2_, ...), custom_call_target="tpu_custom_call" | custom-call | bytes 131072000 | tf_op jit(solution)/shard_map/pallas_call | solution.py:242
  1741.9 6.1 shard_map.43.refs_9_
  1748.0 8.5 shard_map.44.refs_9_
  1756.5 1.9 collective-permute-start.41
  1758.4 2.1 collective-permute-start.42
  1760.5 1.4 collective-permute-start.43
  1762.0 2.3 collective-permute-start.44
  1764.3 41.9 %shard_map.45.refs_9_ = bf16[80,2,320,256]{3,2,1,0:T(8,128)(2,1)} custom-call(s32[81,2]{1,0:T(8,128)} %concatenate.3.counts_ref, bf16[48,160,256]{2,1,0:T(8,128)(2,1)} %get-tuple-element.139.refs_0_, bf16[48,160,256]{2,1,0:T(8,128)(2,1)} %collective-permute-done.31.refs_1_, ...), custom_call_target="tpu_custom_call", output_to_operand_aliasing={{}: (10, {})} | custom-call | flops 10066329600 | bytes 86507520 | tf_op jit(solution)/shard_map/pallas_call | solution.py:299
  1806.2 1.2 collective-permute-start.16
  1807.4 1.8 collective-permute-start.17
  1809.2 1.1 collective-permute-start.18
  1810.3 1.5 collective-permute-start.19
  1811.8 3.4 collective-permute-start.20
  1815.2 15.9 shard_map.46.refs_9_
  1831.1 6.1 shard_map.47.refs_9_
  1838.8 5.1 shard_map.48
  (137 shorter events, 8.5 us)
Async XLA Ops:
  11.7 424.1 %collective-permute-start.21 = (bf16[80,2,160,320]{3,2,1,0:T(8,128)(2,1)}, bf16[80,2,160,320]{3,2,1,0:T(8,128)(2,1)}, u32[]{:S(2)}, u32[]{:S(2)}) collective-permute-start(bf16[80,2,160,320]{3,2,1,0:T(8,128)(2,1)} %refs_0_), channel_id=1, source_target_pairs={{0,2},{1,3},{2,0},{3,1},{4,6},{5,7},{6,4},{7,5},{8,10},{9,11},{10,... | collective-permute-start | bytes 49152008 | tf_op jit(solution)/shard_map/ppermute | solution.py:133
  12.3 1634.5 %collective-permute-start.22 = (bf16[80,2,160,320]{3,2,1,0:T(8,128)(2,1)}, bf16[80,2,160,320]{3,2,1,0:T(8,128)(2,1)}, u32[]{:S(2)}, u32[]{:S(2)}) collective-permute-start(bf16[80,2,160,320]{3,2,1,0:T(8,128)(2,1)} %refs_0_), channel_id=1, source_target_pairs={{0,1},{1,0},{2,3},{3,2},{4,5},{5,4},{6,7},{7,6},{8,9},{9,8},{10,11... | collective-permute-start | bytes 49152008 | tf_op jit(solution)/shard_map/ppermute | solution.py:133
  435.9 1223.5 %collective-permute-start.23 = (bf16[80,2,160,320]{3,2,1,0:T(8,128)(2,1)}, bf16[80,2,160,320]{3,2,1,0:T(8,128)(2,1)}, u32[]{:S(2)}, u32[]{:S(2)}) collective-permute-start(bf16[80,2,160,320]{3,2,1,0:T(8,128)(2,1)} %collective-permute-done.21.refs_1_), channel_id=1, source_target_pairs={{0,1},{1,0},{2,3},{3,2},{4,5},{5,4},{6,7},{7,6},{8,9},{9,8},{10,11... | collective-permute-start | bytes 49152008 | tf_op jit(solution)/shard_map/ppermute | solution.py:133
  435.9 10.2 collective-permute-start.24
  436.6 12.2 collective-permute-start.25
  438.2 23.5 %collective-permute-start.26 = (bf16[4,160,256]{2,1,0:T(8,128)(2,1)S(1)}, bf16[4,160,256]{2,1,0:T(8,128)(2,1)S(1)}, u32[]{:S(2)}, u32[]{:S(2)}) collective-permute-start(bf16[4,160,256]{2,1,0:T(8,128)(2,1)S(1)} %copy.28), channel_id=1, source_target_pairs={{0,12},{4,8},{8,4},{12,0},{16,28},{20,24},{24,20},{28,16},{1,13},{... | collective-permute-start | bytes 983048 | tf_op jit(solution)/shard_map/ppermute | solution.py:363
  446.1 32.5 %collective-permute-start.27 = (bf16[4,160,256]{2,1,0:T(8,128)(2,1)S(1)}, bf16[4,160,256]{2,1,0:T(8,128)(2,1)S(1)}, u32[]{:S(2)}, u32[]{:S(2)}) collective-permute-start(bf16[4,160,256]{2,1,0:T(8,128)(2,1)S(1)} %copy.32), channel_id=1, source_target_pairs={{0,16},{4,20},{8,24},{12,28},{16,0},{20,4},{24,8},{28,12},{1,17},{... | collective-permute-start | bytes 983048 | tf_op jit(solution)/shard_map/ppermute | solution.py:363
  448.8 29.9 %copy-start.11 = (bf16[4,160,256]{2,1,0:T(8,128)(2,1)}, bf16[4,160,256]{2,1,0:T(8,128)(2,1)S(1)}, u32[]{:S(2)}) copy-start(bf16[4,160,256]{2,1,0:T(8,128)(2,1)S(1)} %collective-permute-done.25.refs_2_) | copy-start | bytes 983044
  448.8 88.0 %collective-permute-start.28 = (bf16[4,160,256]{2,1,0:T(8,128)(2,1)S(1)}, bf16[4,160,256]{2,1,0:T(8,128)(2,1)S(1)}, u32[]{:S(2)}, u32[]{:S(2)}) collective-permute-start(bf16[4,160,256]{2,1,0:T(8,128)(2,1)S(1)} %copy.33), channel_id=1, source_target_pairs={{0,20},{4,16},{8,28},{12,24},{16,4},{20,0},{24,12},{28,8},{1,21},{... | collective-permute-start | bytes 983048 | tf_op jit(solution)/shard_map/ppermute | solution.py:363
  461.7 76.7 %collective-permute-start.29 = (bf16[4,160,256]{2,1,0:T(8,128)(2,1)S(1)}, bf16[4,160,256]{2,1,0:T(8,128)(2,1)S(1)}, u32[]{:S(2)}, u32[]{:S(2)}) collective-permute-start(bf16[4,160,256]{2,1,0:T(8,128)(2,1)S(1)} %copy.34), channel_id=1, source_target_pairs={{0,24},{4,28},{8,16},{12,20},{16,8},{20,12},{24,0},{28,4},{1,25},{... | collective-permute-start | bytes 983048 | tf_op jit(solution)/shard_map/ppermute | solution.py:363
  479.4 59.0 %collective-permute-start.30 = (bf16[4,160,256]{2,1,0:T(8,128)(2,1)S(1)}, bf16[4,160,256]{2,1,0:T(8,128)(2,1)S(1)}, u32[]{:S(2)}, u32[]{:S(2)}) collective-permute-start(bf16[4,160,256]{2,1,0:T(8,128)(2,1)S(1)} %copy.35), channel_id=1, source_target_pairs={{0,28},{4,24},{8,20},{12,16},{16,12},{20,8},{24,4},{28,0},{1,29},{... | collective-permute-start | bytes 983048 | tf_op jit(solution)/shard_map/ppermute | solution.py:363
  536.8 25.6 %copy-start.14 = (bf16[4,160,256]{2,1,0:T(8,128)(2,1)}, bf16[4,160,256]{2,1,0:T(8,128)(2,1)S(1)}, u32[]{:S(2)}) copy-start(bf16[4,160,256]{2,1,0:T(8,128)(2,1)S(1)} %collective-permute-done.28.refs_5_) | copy-start | bytes 983044
  536.8 12.7 collective-permute-start
  538.4 24.1 %collective-permute-start.1 = (bf16[6,160,256]{2,1,0:T(8,128)(2,1)}, bf16[6,160,256]{2,1,0:T(8,128)(2,1)S(1)}, u32[]{:S(2)}, u32[]{:S(2)}) collective-permute-start(bf16[6,160,256]{2,1,0:T(8,128)(2,1)} %get-tuple-element.99), channel_id=1, source_target_pairs={{0,8},{4,12},{8,0},{12,4},{16,24},{20,28},{24,16},{28,20},{1,9},{5... | collective-permute-start | bytes 1474568 | tf_op jit(solution)/shard_map/ppermute | solution.py:363
  539.9 64.0 %collective-permute-start.2 = (bf16[6,160,256]{2,1,0:T(8,128)(2,1)}, bf16[6,160,256]{2,1,0:T(8,128)(2,1)S(1)}, u32[]{:S(2)}, u32[]{:S(2)}) collective-permute-start(bf16[6,160,256]{2,1,0:T(8,128)(2,1)} %get-tuple-element.100), channel_id=1, source_target_pairs={{0,12},{4,8},{8,4},{12,0},{16,28},{20,24},{24,20},{28,16},{1,13},{... | collective-permute-start | bytes 1474568 | tf_op jit(solution)/shard_map/ppermute | solution.py:363
  549.5 54.8 %collective-permute-start.3 = (bf16[6,160,256]{2,1,0:T(8,128)(2,1)}, bf16[6,160,256]{2,1,0:T(8,128)(2,1)S(1)}, u32[]{:S(2)}, u32[]{:S(2)}) collective-permute-start(bf16[6,160,256]{2,1,0:T(8,128)(2,1)} %get-tuple-element.101), channel_id=1, source_target_pairs={{0,16},{4,20},{8,24},{12,28},{16,0},{20,4},{24,8},{28,12},{1,17},{... | collective-permute-start | bytes 1474568 | tf_op jit(solution)/shard_map/ppermute | solution.py:363
  563.2 39.9 %copy-start.2 = (bf16[4,160,256]{2,0,1:T(4,128)(2,1)S(1)}, bf16[4,160,256]{2,0,1:T(4,128)(2,1)}, u32[]{:S(2)}) copy-start(bf16[4,160,256]{2,0,1:T(4,128)(2,1)} %get-tuple-element.161) | copy-start | bytes 983044
  563.2 43.2 %copy-start.29 = (bf16[6,160,256]{2,1,0:T(8,128)(2,1)S(1)}, bf16[6,160,256]{2,1,0:T(8,128)(2,1)}, u32[]{:S(2)}) copy-start(bf16[6,160,256]{2,1,0:T(8,128)(2,1)} %get-tuple-element.104) | copy-start | bytes 1474564
  563.3 43.2 %collective-permute-start.4 = (bf16[6,160,256]{2,1,0:T(8,128)(2,1)}, bf16[6,160,256]{2,1,0:T(8,128)(2,1)S(1)}, u32[]{:S(2)}, u32[]{:S(2)}) collective-permute-start(bf16[6,160,256]{2,1,0:T(8,128)(2,1)} %get-tuple-element.102), channel_id=1, source_target_pairs={{0,20},{4,16},{8,28},{12,24},{16,4},{20,0},{24,12},{28,8},{1,21},{... | collective-permute-start | bytes 1474568 | tf_op jit(solution)/shard_map/ppermute | solution.py:363
  603.9 19.0 %copy-start.5 = (bf16[6,160,256]{2,1,0:T(8,128)(2,1)}, bf16[6,160,256]{2,1,0:T(8,128)(2,1)S(1)}, u32[]{:S(2)}) copy-start(bf16[6,160,256]{2,1,0:T(8,128)(2,1)S(1)} %collective-permute-done.2.refs_3_) | copy-start | bytes 1474564
  603.9 209.5 %collective-permute-start.31 = (bf16[48,160,256]{2,1,0:T(8,128)(2,1)}, bf16[48,160,256]{2,1,0:T(8,128)(2,1)}, u32[]{:S(2)}, u32[]{:S(2)}) collective-permute-start(bf16[48,160,256]{2,1,0:T(8,128)(2,1)} %get-tuple-element.140), channel_id=1, source_target_pairs={{0,4},{4,0},{8,12},{12,8},{16,20},{20,16},{24,28},{28,24},{1,5},{5... | collective-permute-start | bytes 11796488 | tf_op jit(solution)/shard_map/ppermute | solution.py:363
  604.3 18.6 %copy-start.6 = (bf16[6,160,256]{2,1,0:T(8,128)(2,1)}, bf16[6,160,256]{2,1,0:T(8,128)(2,1)S(1)}, u32[]{:S(2)}) copy-start(bf16[6,160,256]{2,1,0:T(8,128)(2,1)S(1)} %collective-permute-done.3.refs_4_) | copy-start | bytes 1474564
  604.3 18.6 %collective-permute-start.5 = (bf16[6,160,256]{2,1,0:T(8,128)(2,1)}, bf16[6,160,256]{2,1,0:T(8,128)(2,1)S(1)}, u32[]{:S(2)}, u32[]{:S(2)}) collective-permute-start(bf16[6,160,256]{2,1,0:T(8,128)(2,1)} %get-tuple-element.103), channel_id=1, source_target_pairs={{0,24},{4,28},{8,16},{12,20},{16,8},{20,12},{24,0},{28,4},{1,25},{... | collective-permute-start | bytes 1474568 | tf_op jit(solution)/shard_map/ppermute | solution.py:363
  606.4 16.5 collective-permute-start.6
  623.0 759.8 %copy-start.8 = (bf16[6,160,256]{2,1,0:T(8,128)(2,1)}, bf16[6,160,256]{2,1,0:T(8,128)(2,1)S(1)}, u32[]{:S(2)}) copy-start(bf16[6,160,256]{2,1,0:T(8,128)(2,1)S(1)} %collective-permute-done.5.refs_6_) | copy-start | bytes 1474564
  623.0 759.8 %copy-start.9 = (bf16[6,160,256]{2,1,0:T(8,128)(2,1)}, bf16[6,160,256]{2,1,0:T(8,128)(2,1)S(1)}, u32[]{:S(2)}) copy-start(bf16[6,160,256]{2,1,0:T(8,128)(2,1)S(1)} %collective-permute-done.6.refs_7_) | copy-start | bytes 1474564
  623.0 91.0 %collective-permute-start.7 = (bf16[16,160,256]{2,1,0:T(8,128)(2,1)}, bf16[16,160,256]{2,1,0:T(8,128)(2,1)}, u32[]{:S(2)}, u32[]{:S(2)}) collective-permute-start(bf16[16,160,256]{2,1,0:T(8,128)(2,1)} %get-tuple-element.106), channel_id=1, source_target_pairs={{0,4},{4,0},{8,12},{12,8},{16,20},{20,16},{24,28},{28,24},{1,5},{5... | collective-permute-start | bytes 3932168 | tf_op jit(solution)/shard_map/ppermute | solution.py:363
  623.5 101.9 %collective-permute-start.8 = (bf16[16,160,256]{2,1,0:T(8,128)(2,1)}, bf16[16,160,256]{2,1,0:T(8,128)(2,1)}, u32[]{:S(2)}, u32[]{:S(2)}) collective-permute-start(bf16[16,160,256]{2,1,0:T(8,128)(2,1)} %get-tuple-element.107), channel_id=1, source_target_pairs={{0,8},{4,12},{8,0},{12,4},{16,24},{20,28},{24,16},{28,20},{1,9},{5... | collective-permute-start | bytes 3932168 | tf_op jit(solution)/shard_map/ppermute | solution.py:363
  713.9 99.5 %collective-permute-start.9 = (bf16[16,160,256]{2,1,0:T(8,128)(2,1)}, bf16[16,160,256]{2,1,0:T(8,128)(2,1)}, u32[]{:S(2)}, u32[]{:S(2)}) collective-permute-start(bf16[16,160,256]{2,1,0:T(8,128)(2,1)} %get-tuple-element.108), channel_id=1, source_target_pairs={{0,12},{4,8},{8,4},{12,0},{16,28},{20,24},{24,20},{28,16},{1,13},{... | collective-permute-start | bytes 3932168 | tf_op jit(solution)/shard_map/ppermute | solution.py:363
  725.4 88.0 %collective-permute-start.10 = (bf16[16,160,256]{2,1,0:T(8,128)(2,1)}, bf16[16,160,256]{2,1,0:T(8,128)(2,1)}, u32[]{:S(2)}, u32[]{:S(2)}) collective-permute-start(bf16[16,160,256]{2,1,0:T(8,128)(2,1)} %get-tuple-element.109), channel_id=1, source_target_pairs={{0,16},{4,20},{8,24},{12,28},{16,0},{20,4},{24,8},{28,12},{1,17},{... | collective-permute-start | bytes 3932168 | tf_op jit(solution)/shard_map/ppermute | solution.py:363
  813.4 149.9 %collective-permute-start.32 = (bf16[48,160,256]{2,1,0:T(8,128)(2,1)}, bf16[48,160,256]{2,1,0:T(8,128)(2,1)}, u32[]{:S(2)}, u32[]{:S(2)}) collective-permute-start(bf16[48,160,256]{2,1,0:T(8,128)(2,1)} %get-tuple-element.141), channel_id=1, source_target_pairs={{0,8},{4,12},{8,0},{12,4},{16,24},{20,28},{24,16},{28,20},{1,9},{5... | collective-permute-start | bytes 11796488 | tf_op jit(solution)/shard_map/ppermute | solution.py:363
  813.4 243.5 %collective-permute-start.33 = (bf16[48,160,256]{2,1,0:T(8,128)(2,1)}, bf16[48,160,256]{2,1,0:T(8,128)(2,1)}, u32[]{:S(2)}, u32[]{:S(2)}) collective-permute-start(bf16[48,160,256]{2,1,0:T(8,128)(2,1)} %get-tuple-element.142), channel_id=1, source_target_pairs={{0,12},{4,8},{8,4},{12,0},{16,28},{20,24},{24,20},{28,16},{1,13},{... | collective-permute-start | bytes 11796488 | tf_op jit(solution)/shard_map/ppermute | solution.py:363
  813.5 254.2 %collective-permute-start.34 = (bf16[48,160,256]{2,1,0:T(8,128)(2,1)}, bf16[48,160,256]{2,1,0:T(8,128)(2,1)}, u32[]{:S(2)}, u32[]{:S(2)}) collective-permute-start(bf16[48,160,256]{2,1,0:T(8,128)(2,1)} %get-tuple-element.143), channel_id=1, source_target_pairs={{0,16},{4,20},{8,24},{12,28},{16,0},{20,4},{24,8},{28,12},{1,17},{... | collective-permute-start | bytes 11796488 | tf_op jit(solution)/shard_map/ppermute | solution.py:363
  963.3 419.5 %collective-permute-start.35 = (bf16[48,160,256]{2,1,0:T(8,128)(2,1)}, bf16[48,160,256]{2,1,0:T(8,128)(2,1)}, u32[]{:S(2)}, u32[]{:S(2)}) collective-permute-start(bf16[48,160,256]{2,1,0:T(8,128)(2,1)} %get-tuple-element.144), channel_id=1, source_target_pairs={{0,20},{4,16},{8,28},{12,24},{16,4},{20,0},{24,12},{28,8},{1,21},{... | collective-permute-start | bytes 11796488 | tf_op jit(solution)/shard_map/ppermute | solution.py:363
  1056.9 325.9 %collective-permute-start.36 = (bf16[48,160,256]{2,1,0:T(8,128)(2,1)}, bf16[48,160,256]{2,1,0:T(8,128)(2,1)}, u32[]{:S(2)}, u32[]{:S(2)}) collective-permute-start(bf16[48,160,256]{2,1,0:T(8,128)(2,1)} %get-tuple-element.145), channel_id=1, source_target_pairs={{0,24},{4,28},{8,16},{12,20},{16,8},{20,12},{24,0},{28,4},{1,25},{... | collective-permute-start | bytes 11796488 | tf_op jit(solution)/shard_map/ppermute | solution.py:363
  1067.7 320.2 %collective-permute-start.37 = (bf16[48,160,256]{2,1,0:T(8,128)(2,1)}, bf16[48,160,256]{2,1,0:T(8,128)(2,1)}, u32[]{:S(2)}, u32[]{:S(2)}) collective-permute-start(bf16[48,160,256]{2,1,0:T(8,128)(2,1)} %get-tuple-element.146), channel_id=1, source_target_pairs={{0,28},{4,24},{8,20},{12,16},{16,12},{20,8},{24,4},{28,0},{1,29},{... | collective-permute-start | bytes 11796488 | tf_op jit(solution)/shard_map/ppermute | solution.py:363
  1382.8 238.6 %collective-permute-start.11 = (bf16[16,160,256]{2,1,0:T(8,128)(2,1)}, bf16[16,160,256]{2,1,0:T(8,128)(2,1)S(1)}, u32[]{:S(2)}, u32[]{:S(2)}) collective-permute-start(bf16[16,160,256]{2,1,0:T(8,128)(2,1)} %get-tuple-element.110), channel_id=1, source_target_pairs={{0,20},{4,16},{8,28},{12,24},{16,4},{20,0},{24,12},{28,8},{1,21},{... | collective-permute-start | bytes 3932168 | tf_op jit(solution)/shard_map/ppermute | solution.py:363
  1382.8 238.7 %collective-permute-start.12 = (bf16[16,160,256]{2,1,0:T(8,128)(2,1)}, bf16[16,160,256]{2,1,0:T(8,128)(2,1)S(1)}, u32[]{:S(2)}, u32[]{:S(2)}) collective-permute-start(bf16[16,160,256]{2,1,0:T(8,128)(2,1)} %get-tuple-element.111), channel_id=1, source_target_pairs={{0,24},{4,28},{8,16},{12,20},{16,8},{20,12},{24,0},{28,4},{1,25},{... | collective-permute-start | bytes 3932168 | tf_op jit(solution)/shard_map/ppermute | solution.py:363
  1387.8 258.4 %collective-permute-start.13 = (bf16[16,160,256]{2,1,0:T(8,128)(2,1)}, bf16[16,160,256]{2,1,0:T(8,128)(2,1)}, u32[]{:S(2)}, u32[]{:S(2)}) collective-permute-start(bf16[16,160,256]{2,1,0:T(8,128)(2,1)} %get-tuple-element.112), channel_id=1, source_target_pairs={{0,28},{4,24},{8,20},{12,16},{16,12},{20,8},{24,4},{28,0},{1,29},{... | collective-permute-start | bytes 3932168 | tf_op jit(solution)/shard_map/ppermute | solution.py:363
  1621.4 23.4 %copy-start = (bf16[16,160,256]{2,1,0:T(8,128)(2,1)}, bf16[16,160,256]{2,1,0:T(8,128)(2,1)S(1)}, u32[]{:S(2)}) copy-start(bf16[16,160,256]{2,1,0:T(8,128)(2,1)S(1)} %collective-permute-done.11.refs_5_) | copy-start | bytes 3932164
  1621.4 139.1 %collective-permute-start.38 = (bf16[4,160,256]{2,1,0:T(8,128)(2,1)}, bf16[4,160,256]{2,1,0:T(8,128)(2,1)}, u32[]{:S(2)}, u32[]{:S(2)}) collective-permute-start(bf16[4,160,256]{2,1,0:T(8,128)(2,1)} %get-tuple-element.148), channel_id=1, source_target_pairs={{0,4},{4,0},{8,12},{12,8},{16,20},{20,16},{24,28},{28,24},{1,5},{5... | collective-permute-start | bytes 983048 | tf_op jit(solution)/shard_map/ppermute | solution.py:363
  1621.5 23.4 %copy-start.1 = (bf16[16,160,256]{2,1,0:T(8,128)(2,1)}, bf16[16,160,256]{2,1,0:T(8,128)(2,1)S(1)}, u32[]{:S(2)}) copy-start(bf16[16,160,256]{2,1,0:T(8,128)(2,1)S(1)} %collective-permute-done.12.refs_6_) | copy-start | bytes 3932164
  1621.5 140.5 %collective-permute-start.39 = (bf16[4,160,256]{2,1,0:T(8,128)(2,1)}, bf16[4,160,256]{2,1,0:T(8,128)(2,1)}, u32[]{:S(2)}, u32[]{:S(2)}) collective-permute-start(bf16[4,160,256]{2,1,0:T(8,128)(2,1)} %get-tuple-element.149), channel_id=1, source_target_pairs={{0,8},{4,12},{8,0},{12,4},{16,24},{20,28},{24,16},{28,20},{1,9},{5... | collective-permute-start | bytes 983048 | tf_op jit(solution)/shard_map/ppermute | solution.py:363
  1646.2 110.3 %collective-permute-start.14 = (bf16[2,160,256]{2,1,0:T(8,128)(2,1)}, bf16[2,160,256]{2,1,0:T(8,128)(2,1)S(1)}, u32[]{:S(2)}, u32[]{:S(2)}) collective-permute-start(bf16[2,160,256]{2,1,0:T(8,128)(2,1)} %get-tuple-element.114), channel_id=1, source_target_pairs={{0,4},{4,0},{8,12},{12,8},{16,20},{20,16},{24,28},{28,24},{1,5},{5... | collective-permute-start | bytes 491528 | tf_op jit(solution)/shard_map/ppermute | solution.py:363
  1646.9 111.5 %collective-permute-start.15 = (bf16[2,160,256]{2,1,0:T(8,128)(2,1)}, bf16[2,160,256]{2,1,0:T(8,128)(2,1)S(1)}, u32[]{:S(2)}, u32[]{:S(2)}) collective-permute-start(bf16[2,160,256]{2,1,0:T(8,128)(2,1)} %get-tuple-element.115), channel_id=1, source_target_pairs={{0,8},{4,12},{8,0},{12,4},{16,24},{20,28},{24,16},{28,20},{1,9},{5... | collective-permute-start | bytes 491528 | tf_op jit(solution)/shard_map/ppermute | solution.py:363
  1659.4 146.8 %collective-permute-start.40 = (bf16[4,160,256]{2,1,0:T(8,128)(2,1)}, bf16[4,160,256]{2,1,0:T(8,128)(2,1)}, u32[]{:S(2)}, u32[]{:S(2)}) collective-permute-start(bf16[4,160,256]{2,1,0:T(8,128)(2,1)} %get-tuple-element.150), channel_id=1, source_target_pairs={{0,12},{4,8},{8,4},{12,0},{16,28},{20,24},{24,20},{28,16},{1,13},{... | collective-permute-start | bytes 983048 | tf_op jit(solution)/shard_map/ppermute | solution.py:363
  1756.5 52.8 %copy-start.36 = (bf16[2,160,256]{2,1,0:T(8,128)(2,1)S(1)}, bf16[2,160,256]{2,1,0:T(8,128)(2,1)}, u32[]{:S(2)}) copy-start(bf16[2,160,256]{2,1,0:T(8,128)(2,1)} %get-tuple-element.118) | copy-start | bytes 491524
  1756.5 53.8 %copy-start.35 = (bf16[2,160,256]{2,1,0:T(8,128)(2,1)S(1)}, bf16[2,160,256]{2,1,0:T(8,128)(2,1)}, u32[]{:S(2)}) copy-start(bf16[2,160,256]{2,1,0:T(8,128)(2,1)} %get-tuple-element.119) | copy-start | bytes 491524
  1756.5 55.3 %copy-start.34 = (bf16[2,160,256]{2,1,0:T(8,128)(2,1)S(1)}, bf16[2,160,256]{2,1,0:T(8,128)(2,1)}, u32[]{:S(2)}) copy-start(bf16[2,160,256]{2,1,0:T(8,128)(2,1)} %get-tuple-element.120) | copy-start | bytes 491524
  1756.5 49.7 %copy-start.22 = (bf16[2,160,256]{2,1,0:T(8,128)(2,1)}, bf16[2,160,256]{2,1,0:T(8,128)(2,1)S(1)}, u32[]{:S(2)}) copy-start(bf16[2,160,256]{2,1,0:T(8,128)(2,1)S(1)} %collective-permute-done.14.refs_1_) | copy-start | bytes 491524
  1756.5 50.9 %collective-permute-start.41 = (bf16[4,160,256]{2,1,0:T(8,128)(2,1)S(1)}, bf16[4,160,256]{2,1,0:T(8,128)(2,1)S(1)}, u32[]{:S(2)}, u32[]{:S(2)}) collective-permute-start(bf16[4,160,256]{2,1,0:T(8,128)(2,1)S(1)} %copy-done.33), channel_id=1, source_target_pairs={{0,16},{4,20},{8,24},{12,28},{16,0},{20,4},{24,8},{28,12},{1,17},{... | collective-permute-start | bytes 983048 | tf_op jit(solution)/shard_map/ppermute | solution.py:363
  1758.4 47.8 %copy-start.23 = (bf16[2,160,256]{2,1,0:T(8,128)(2,1)}, bf16[2,160,256]{2,1,0:T(8,128)(2,1)S(1)}, u32[]{:S(2)}) copy-start(bf16[2,160,256]{2,1,0:T(8,128)(2,1)S(1)} %collective-permute-done.15.refs_2_) | copy-start | bytes 491524
  1758.4 50.8 %collective-permute-start.42 = (bf16[4,160,256]{2,1,0:T(8,128)(2,1)S(1)}, bf16[4,160,256]{2,1,0:T(8,128)(2,1)S(1)}, u32[]{:S(2)}, u32[]{:S(2)}) collective-permute-start(bf16[4,160,256]{2,1,0:T(8,128)(2,1)S(1)} %copy-done.32), channel_id=1, source_target_pairs={{0,20},{4,16},{8,28},{12,24},{16,4},{20,0},{24,12},{28,8},{1,21},{... | collective-permute-start | bytes 983048 | tf_op jit(solution)/shard_map/ppermute | solution.py:363
  1760.5 49.8 %collective-permute-start.43 = (bf16[4,160,256]{2,1,0:T(8,128)(2,1)S(1)}, bf16[4,160,256]{2,1,0:T(8,128)(2,1)S(1)}, u32[]{:S(2)}, u32[]{:S(2)}) collective-permute-start(bf16[4,160,256]{2,1,0:T(8,128)(2,1)S(1)} %copy-done.31), channel_id=1, source_target_pairs={{0,24},{4,28},{8,16},{12,20},{16,8},{20,12},{24,0},{28,4},{1,25},{... | collective-permute-start | bytes 983048 | tf_op jit(solution)/shard_map/ppermute | solution.py:363
  1762.0 49.8 %collective-permute-start.44 = (bf16[4,160,256]{2,1,0:T(8,128)(2,1)S(1)}, bf16[4,160,256]{2,1,0:T(8,128)(2,1)S(1)}, u32[]{:S(2)}, u32[]{:S(2)}) collective-permute-start(bf16[4,160,256]{2,1,0:T(8,128)(2,1)S(1)} %copy-done.30), channel_id=1, source_target_pairs={{0,28},{4,24},{8,20},{12,16},{16,12},{20,8},{24,4},{28,0},{1,29},{... | collective-permute-start | bytes 983048 | tf_op jit(solution)/shard_map/ppermute | solution.py:363
  1806.2 31.1 %collective-permute-start.16 = (bf16[2,160,256]{2,1,0:T(8,128)(2,1)}, bf16[2,160,256]{2,1,0:T(8,128)(2,1)S(1)}, u32[]{:S(2)}, u32[]{:S(2)}) collective-permute-start(bf16[2,160,256]{2,1,0:T(8,128)(2,1)} %get-tuple-element.116), channel_id=1, source_target_pairs={{0,12},{4,8},{8,4},{12,0},{16,28},{20,24},{24,20},{28,16},{1,13},{... | collective-permute-start | bytes 491528 | tf_op jit(solution)/shard_map/ppermute | solution.py:363
  1807.4 23.7 %copy-start.17 = (bf16[4,160,256]{2,1,0:T(8,128)(2,1)}, bf16[4,160,256]{2,1,0:T(8,128)(2,1)S(1)}, u32[]{:S(2)}) copy-start(bf16[4,160,256]{2,1,0:T(8,128)(2,1)S(1)} %collective-permute-done.41.refs_4_) | copy-start | bytes 983044
  1807.4 29.9 %collective-permute-start.17 = (bf16[2,160,256]{2,1,0:T(8,128)(2,1)}, bf16[2,160,256]{2,1,0:T(8,128)(2,1)S(1)}, u32[]{:S(2)}, u32[]{:S(2)}) collective-permute-start(bf16[2,160,256]{2,1,0:T(8,128)(2,1)} %get-tuple-element.117), channel_id=1, source_target_pairs={{0,16},{4,20},{8,24},{12,28},{16,0},{20,4},{24,8},{28,12},{1,17},{... | collective-permute-start | bytes 491528 | tf_op jit(solution)/shard_map/ppermute | solution.py:363
  1809.2 21.9 %copy-start.18 = (bf16[4,160,256]{2,1,0:T(8,128)(2,1)}, bf16[4,160,256]{2,1,0:T(8,128)(2,1)S(1)}, u32[]{:S(2)}) copy-start(bf16[4,160,256]{2,1,0:T(8,128)(2,1)S(1)} %collective-permute-done.42.refs_5_) | copy-start | bytes 983044
  1809.2 28.1 %collective-permute-start.18 = (bf16[2,160,256]{2,1,0:T(8,128)(2,1)S(1)}, bf16[2,160,256]{2,1,0:T(8,128)(2,1)S(1)}, u32[]{:S(2)}, u32[]{:S(2)}) collective-permute-start(bf16[2,160,256]{2,1,0:T(8,128)(2,1)S(1)} %copy-done.36), channel_id=1, source_target_pairs={{0,20},{4,16},{8,28},{12,24},{16,4},{20,0},{24,12},{28,8},{1,21},{... | collective-permute-start | bytes 491528 | tf_op jit(solution)/shard_map/ppermute | solution.py:363
  1810.3 20.8 %copy-start.19 = (bf16[4,160,256]{2,1,0:T(8,128)(2,1)}, bf16[4,160,256]{2,1,0:T(8,128)(2,1)S(1)}, u32[]{:S(2)}) copy-start(bf16[4,160,256]{2,1,0:T(8,128)(2,1)S(1)} %collective-permute-done.43.refs_6_) | copy-start | bytes 983044
  1810.3 27.0 %collective-permute-start.19 = (bf16[2,160,256]{2,1,0:T(8,128)(2,1)S(1)}, bf16[2,160,256]{2,1,0:T(8,128)(2,1)S(1)}, u32[]{:S(2)}, u32[]{:S(2)}) collective-permute-start(bf16[2,160,256]{2,1,0:T(8,128)(2,1)S(1)} %copy-done.35), channel_id=1, source_target_pairs={{0,24},{4,28},{8,16},{12,20},{16,8},{20,12},{24,0},{28,4},{1,25},{... | collective-permute-start | bytes 491528 | tf_op jit(solution)/shard_map/ppermute | solution.py:363
  1811.8 19.3 %copy-start.20 = (bf16[4,160,256]{2,1,0:T(8,128)(2,1)}, bf16[4,160,256]{2,1,0:T(8,128)(2,1)S(1)}, u32[]{:S(2)}) copy-start(bf16[4,160,256]{2,1,0:T(8,128)(2,1)S(1)} %collective-permute-done.44.refs_7_) | copy-start | bytes 983044
  1811.8 25.5 %collective-permute-start.20 = (bf16[2,160,256]{2,1,0:T(8,128)(2,1)S(1)}, bf16[2,160,256]{2,1,0:T(8,128)(2,1)S(1)}, u32[]{:S(2)}, u32[]{:S(2)}) collective-permute-start(bf16[2,160,256]{2,1,0:T(8,128)(2,1)S(1)} %copy-done.34), channel_id=1, source_target_pairs={{0,28},{4,24},{8,20},{12,16},{16,12},{20,8},{24,4},{28,0},{1,29},{... | collective-permute-start | bytes 491528 | tf_op jit(solution)/shard_map/ppermute | solution.py:363
  (18 other events, 123.1 us)
